TPU v7x, 32 devices: a whole 2x2x4 slice. The times are simulated.
32 devices in a mesh: band: 16 (over z, y, core), slab: 2 (over x).
Axes of the slice: x: 2, y: 2, z: 4, core: 2. Of those that a mesh axis runs over, the one named last changes fastest.
Arguments:
- orbitals: bfloat16 [32, 32, 4096], P('band', 'slab'), may hold values from -6 to 6
- occupation: bfloat16 [32], P('band'), may hold values from 0.25 to 1
Outputs:
- exchange_field: float32 [32, 32, 4096], P('band', 'slab')
All inputs are finite; a program needn't handle non-finite values.
Results may differ from a plain program's by a relative error of at most 0.001.
Values may be sent and summed in bfloat16 or wider, within the bound.
A program may use at most 64 MiB of HBM per device.

v0:
```python
import functools
import math

import jax
import jax.numpy as jnp
from jax import lax
from jax.experimental import pallas as pl
from jax.experimental.pallas import tpu as pltpu
from jax.sharding import PartitionSpec as P

NZ = 64
STEPS = 3
LANES = 128
WIDTH = 2
UNROLL = 8
MESH = pl.DeviceIdType.MESH


screening = 0.5
ratio_mid = (12.0 + 2.0 * screening) / 12.0
root_term = math.sqrt(ratio_mid * ratio_mid - 1.0)
decay_ratio = ratio_mid - root_term
coeff_zero = 1.0 / (6.0 * root_term)
coeff_one = -2.0 * decay_ratio * coeff_zero
coeff_two = 2.0 * decay_ratio * decay_ratio * coeff_zero

scale = coeff_two / 18.0
inner = -coeff_one / 6.0 / scale
outer = (coeff_zero - coeff_two) / scale


def loop(count, body, unroll=1):
    lax.fori_loop(0, count, lambda i, c: (body(i), c)[1], 0, unroll=unroll)


def lane_tile(t):
    return pl.ds(pl.multiple_of(t * LANES, LANES), LANES)


def kernel(n_band, n_slab, orb_ref, occ_ref, out_ref, slots, edges, halos, own, own_moved, vis,
           weighted, dens, turned, part, inner_field, load_sem, send_sem, recv_sem, edge_send, edge_recv):
    orbs, planes, cells = orb_ref.shape
    tiles = cells // LANES
    ext = vis.shape[1]
    mine = STEPS
    band, slab = lax.axis_index("band"), lax.axis_index("slab")
    odd = lax.rem(band, 2)

    def at(by, side=0):
        return {"band": lax.rem(band + by + n_band, n_band), "slab": slab + side}

    sibling = at(1 - 2 * odd)
    has = (slab > 0, slab < n_slab - 1)
    step_of = (-1, 1)
    reach = {mine: 0, 1: 2, 0: 1 + 2 * odd}
    source = {mine: 0, 1: -2, 0: 2 * odd - 3}

    load = pltpu.make_async_copy(orb_ref, slots.at[mine, :, :, :cells], load_sem.at[0])
    load.start()

    barrier = pltpu.get_barrier_semaphore()
    for by in (source[1], source[0]):
        pl.semaphore_signal(barrier, inc=1, device_id=at(by), device_id_type=MESH)
    pl.semaphore_signal(barrier, inc=1, device_id=sibling, device_id_type=MESH)
    for side in range(2):
        @pl.when(has[side])
        def _(side=side):
            for slot in (mine, 1, 0):
                pl.semaphore_signal(barrier, inc=1, device_id=at(source[slot], step_of[side]), device_id_type=MESH)

    load.wait()
    for o in range(orbs):
        value = jnp.broadcast_to(occ_ref[:, o:o + 1].astype(jnp.float32), (planes, LANES))
        slots[mine, o, :, cells:] = value.astype(jnp.bfloat16)

    def cut(k):
        parts = ([], [])
        for h in range(2):
            for o in range(orbs):
                tile = slots[mine, o, :, lane_tile(2 * k + h)].astype(jnp.float32)
                parts[0].append(tile[:WIDTH])
                parts[1].append(tile[planes - WIDTH:])
        for side in range(2):
            edges[side, k] = jnp.concatenate(parts[side], axis=0).astype(jnp.bfloat16)

    loop(tiles // 2, cut, 2)

    for side in range(2):
        @pl.when(jnp.logical_not(has[side]))
        def _(side=side):
            halos[:, side] = jnp.zeros(halos.shape[:1] + halos.shape[2:], jnp.bfloat16)

    sides = has[0].astype(jnp.int32) + has[1].astype(jnp.int32)
    pl.semaphore_wait(barrier, 3 + 3 * sides)

    def edge_copy(side, slot):
        return pltpu.make_async_remote_copy(
            src_ref=edges.at[side], dst_ref=halos.at[slot, 1 - side],
            send_sem=edge_send.at[slot, side], recv_sem=edge_recv.at[slot, 1 - side],
            device_id=at(reach[slot], step_of[side]), device_id_type=MESH)

    def edge_pass(side):
        return pltpu.make_async_remote_copy(
            src_ref=halos.at[1, side], dst_ref=halos.at[2, side],
            send_sem=edge_send.at[2, side], recv_sem=edge_recv.at[2, side],
            device_id=sibling, device_id_type=MESH)

    def edge_wait(side, slot):
        pltpu.make_async_remote_copy(
            src_ref=edges.at[1 - side], dst_ref=halos.at[slot, side],
            send_sem=edge_send.at[slot, 1 - side], recv_sem=edge_recv.at[slot, side],
            device_id=sibling, device_id_type=MESH).wait_recv()

    def block_copy(slot, o):
        return pltpu.make_async_remote_copy(
            src_ref=slots.at[mine, o], dst_ref=slots.at[slot, o], send_sem=send_sem.at[slot, o],
            recv_sem=recv_sem.at[slot, o], device_id=at(reach[slot]), device_id_type=MESH)

    def block_pass(o):
        return pltpu.make_async_remote_copy(
            src_ref=slots.at[1, o], dst_ref=slots.at[2, o], send_sem=send_sem.at[2, o],
            recv_sem=recv_sem.at[2, o], device_id=sibling, device_id_type=MESH)

    def each_side(action):
        for side in range(2):
            pl.when(has[side])(functools.partial(action, side))

    each_side(lambda side: edge_copy(side, mine).start())
    each_side(lambda side: edge_copy(side, 1).start())
    each_side(lambda side: edge_copy(side, 0).start())
    for o in range(orbs):
        block_copy(1, o).start()
        block_copy(0, o).start()

    for i in range(orbs):
        for t in (0, tiles + 1):
            turned[i, t] = jnp.zeros(turned.shape[2:], jnp.float32)
            inner_field[i, t] = jnp.zeros(inner_field.shape[2:], jnp.float32)

    lane = lax.broadcasted_iota(jnp.int32, (1, LANES), 1)
    high = lane >= NZ
    column = lane % NZ
    first_col, last_col = column == 0, column == NZ - 1
    row = lax.broadcasted_iota(jnp.int32, (ext, LANES), 0)
    below = jnp.where(has[0], 1.0, 0.0)
    above = jnp.where(has[1], 1.0, 0.0)
    row_mask = jnp.where(row == WIDTH - 1, below, jnp.where(row == planes + WIDTH, above, 1.0))

    def from_left(mid):
        return pltpu.roll(jnp.where(last_col, 0.0, mid), 1, 1)

    def from_right(mid):
        return pltpu.roll(jnp.where(first_col, 0.0, mid), LANES - 1, 1)

    def pick(rows, h, o):
        value = None
        for q in range(orbs):
            r = (h * orbs + q) * WIDTH
            piece = rows[r:r + WIDTH]
            value = piece if value is None else jnp.where(o == q, piece, value)
        return value

    def widen(slot, o, dst):
        def body(k):
            low = halos[slot, 0, k].astype(jnp.float32)
            up = halos[slot, 1, k].astype(jnp.float32)
            for h in range(2):
                t = 2 * k + h
                dst[t, :WIDTH] = pick(low, h, o)
                dst[t, planes + WIDTH:planes + 2 * WIDTH] = pick(up, h, o)
                dst[t, WIDTH:planes + WIDTH] = slots[slot, o, :, lane_tile(t)].astype(jnp.float32)
        loop(tiles // 2, body, 4)

    def visit(slot, o):
        weight = -scale * slots[slot, o, :, cells:].astype(jnp.float32)
        widen(slot, o, vis)

        def density(t):
            mid = vis[t]
            moved = (pltpu.roll(mid, NZ, 1), from_left(mid), from_right(mid))
            weighted[t] = weight * vis[t, WIDTH:planes + WIDTH]
            for i in range(orbs):
                d = own[i, t] * mid
                dens[i, t, 8:ext + 8] = d
                turn = own_moved[i, 0, t] * moved[0]
                turned[i, t + 1] = turn
                part[i, t] = inner * d + turn + (own_moved[i, 1, t] * moved[1] + own_moved[i, 2, t] * moved[2])

        def once(t):
            for i in range(orbs):
                along = dens[i, t, 7:ext + 7] + dens[i, t, 9:ext + 9]
                u = part[i, t] + along + jnp.where(high, turned[i, t + 2], turned[i, t])
                inner_field[i, t + 1] = u * row_mask

        def twice(t):
            for i in range(orbs):
                mid = inner_field[i, t + 1, WIDTH:planes + WIDTH]
                before = inner_field[i, t, WIDTH:planes + WIDTH]
                after = inner_field[i, t + 2, WIDTH:planes + WIDTH]
                v = inner_field[i, t + 1, WIDTH - 1:planes + WIDTH - 1] + inner_field[i, t + 1, WIDTH + 1:planes + WIDTH + 1]
                v = v + pltpu.roll(mid + jnp.where(high, before, after), NZ, 1)
                v = v + (from_left(mid) + from_right(mid))
                v = v + outer * dens[i, t, 8 + WIDTH:8 + planes + WIDTH]
                out_ref[i, :, lane_tile(t)] += weighted[t] * v

        loop(tiles, density, UNROLL)
        loop(tiles, once, UNROLL)
        loop(tiles, twice, UNROLL)

    each_side(lambda side: edge_wait(side, mine))
    for i in range(orbs):
        widen(mine, i, own.at[i])

    def prepare(t):
        for i in range(orbs):
            mid = own[i, t]
            own_moved[i, 0, t] = pltpu.roll(mid, NZ, 1)
            own_moved[i, 1, t] = from_left(mid)
            own_moved[i, 2, t] = from_right(mid)
            out_ref[i, :, lane_tile(t)] = jnp.zeros((planes, LANES), jnp.float32)

    loop(tiles, prepare, UNROLL)

    if_odd, if_even = [(mine, o) for o in range(orbs)], [(mine, o) for o in range(orbs)]
    if_odd += [(0, o) for o in range(orbs)]
    for o in range(orbs):
        if_odd += [(1, o), (2, o)]
        if_even += [(1, o), (0, o), (2, o)]

    def entry(k, column):
        value = jnp.int32(0)
        for n, (a, b) in enumerate(zip(if_odd, if_even)):
            value = jnp.where(k == n, jnp.where(odd == 1, a[column], b[column]), value)
        return value

    def step(k):
        slot, o = entry(k, 0), entry(k, 1)
        for q in range(STEPS):
            for p in range(orbs):
                @pl.when(jnp.logical_and(slot == q, o == p))
                def _(q=q, p=p):
                    if p == 0:
                        each_side(lambda side: edge_wait(side, q))
                        if q == 1:
                            each_side(lambda side: edge_pass(side).start())
                    (block_pass(p) if q == 2 else block_copy(q, p)).wait_recv()
                    if q == 1:
                        block_pass(p).start()
        visit(slot, o)

    loop(len(if_odd), step)

    for o in range(orbs):
        block_copy(0, o).wait_send()
        block_copy(1, o).wait_send()
        block_pass(o).wait_send()
    for slot in (mine, 1, 0):
        each_side(lambda side: edge_copy(side, slot).wait_send())
    each_side(lambda side: edge_pass(side).wait_send())


def per_device(n_band, n_slab, orbitals, occupation):
    orbs, planes, cells = orbitals.shape
    tiles = cells // LANES
    ext = -(-(planes + 2 * WIDTH) // 8) * 8
    occ = occupation.reshape(1, orbs)
    f32, bf16 = jnp.float32, jnp.bfloat16
    rows = 2 * orbs * WIDTH
    return pl.pallas_call(
        functools.partial(kernel, n_band, n_slab),
        out_shape=jax.ShapeDtypeStruct(orbitals.shape, f32),
        in_specs=[pl.BlockSpec(memory_space=pl.ANY), pl.BlockSpec(memory_space=pltpu.VMEM)],
        out_specs=pl.BlockSpec(memory_space=pltpu.VMEM),
        scratch_shapes=[
            pltpu.VMEM((STEPS + 1, orbs, planes, cells + LANES), bf16),
            pltpu.VMEM((2, tiles // 2, rows, LANES), bf16),
            pltpu.VMEM((STEPS + 1, 2, tiles // 2, rows, LANES), bf16),
            pltpu.VMEM((orbs, tiles, ext, LANES), f32),
            pltpu.VMEM((orbs, 3, tiles, ext, LANES), f32),
            pltpu.VMEM((tiles, ext, LANES), f32),
            pltpu.VMEM((tiles, planes, LANES), f32),
            pltpu.VMEM((orbs, tiles, ext + 16, LANES), f32),
            pltpu.VMEM((orbs, tiles + 2, ext, LANES), f32),
            pltpu.VMEM((orbs, tiles, ext, LANES), f32),
            pltpu.VMEM((orbs, tiles + 2, ext, LANES), f32),
            pltpu.SemaphoreType.DMA((1,)),
            pltpu.SemaphoreType.DMA((STEPS, orbs)),
            pltpu.SemaphoreType.DMA((STEPS, orbs)),
            pltpu.SemaphoreType.DMA((STEPS + 1, 2)),
            pltpu.SemaphoreType.DMA((STEPS + 1, 2)),
        ],
        compiler_params=pltpu.CompilerParams(collective_id=0, has_side_effects=True),
        name="exchange",
    )(orbitals, occ)


def solution(mesh):
    in_specs = (P("band", "slab", None), P("band"))
    out_specs = P("band", "slab", None)
    return jax.shard_map(
        functools.partial(per_device, mesh.shape["band"], mesh.shape["slab"]),
        mesh=mesh, in_specs=in_specs, out_specs=out_specs, check_vma=False,
    )
```

profile of v0, /device:TPU:0, one launch (start us, length us, event | category | flops | bytes accessed | tf_op | source)
XLA Modules:
  0.0 26.2 jit_solution(4555690903893815571)
XLA Ops:
  0.0 24.3 %exchange.1 = f32[2,16,4096]{2,1,0:T(8,128)} custom-call(bf16[2,16,4096]{2,1,0:T(8,128)(2,1)} %orb_ref.1, bf16[1,2]{1,0:T(2,128)(2,1)} %bitcast.1), custom_call_target="tpu_custom_call" | custom-call | tf_op jit(solution)/shard_map/exchange/pallas_call | solution.py:269
  24.4 1.9 %copy.4 = f32[2,16,4096]{2,1,0:T(8,128)} copy(f32[2,16,4096]{2,1,0:T(8,128)} %exchange.1) | data formatting | bytes 1048576
where the time goes:
time: 26.4 us; the launch traced here: 26.2 us
  Pallas kernels  24.3 us (92%)
  local copies, waits for them, and re-layouts  1.87 us (7%)
    pallas_call x1, Pallas kernels, per_device(): pl.pallas_call(functools.partial(kernel, n_band, n_slab), out_shape=jax.S...  24.3 us
    unnamed x1, local copies, waits for them, and re-layouts  1.87 us

commit v1 on v0

v1 whole, which is shorter than its diff:
```python
import functools
import math

import jax
import jax.numpy as jnp
from jax import lax
from jax.experimental import pallas as pl
from jax.experimental.pallas import tpu as pltpu
from jax.sharding import PartitionSpec as P

NZ = 64
STEPS = 3
LANES = 128
WIDTH = 2
PAD = 2
TOP = 8
FLAT = ((0, 0), (0, 1), (0, 2), (1, 0), (2, 0), (1, 1), (1, -1))
WIDE = ((0, 1, 0), (0, 2, 0), (0, 1, 1), (0, 1, -1), (1, 1, 0), (1, -1, 0))
MESH = pl.DeviceIdType.MESH


screening = 0.5
ratio_mid = (12.0 + 2.0 * screening) / 12.0
root_term = math.sqrt(ratio_mid * ratio_mid - 1.0)
decay_ratio = ratio_mid - root_term
coeff_zero = 1.0 / (6.0 * root_term)
coeff_one = -2.0 * decay_ratio * coeff_zero
coeff_two = 2.0 * decay_ratio * decay_ratio * coeff_zero

scale = coeff_two / 18.0
inner = -coeff_one / 6.0 / scale
outer = (coeff_zero - coeff_two) / scale


def loop(count, body, unroll=1):
    lax.fori_loop(0, count, lambda i, c: (body(i), c)[1], 0, unroll=unroll)


def lane_tile(t):
    return pl.ds(pl.multiple_of(t * LANES, LANES), LANES)


def kernel(n_band, n_slab, orb_ref, occ_ref, out_ref, slots, edges, halos, own, vis, gram, wide, centre,
           load_sem, send_sem, recv_sem, edge_send, edge_recv):
    orbs, planes, cells = orb_ref.shape
    tiles = cells // LANES
    half = tiles // 2
    mine = STEPS
    band, slab = lax.axis_index("band"), lax.axis_index("slab")
    odd = lax.rem(band, 2)

    def at(by, side=0):
        return {"band": lax.rem(band + by + n_band, n_band), "slab": slab + side}

    sibling = at(1 - 2 * odd)
    has = (slab > 0, slab < n_slab - 1)
    step_of = (-1, 1)
    reach = {mine: 0, 1: 2, 0: 1 + 2 * odd}
    source = {mine: 0, 1: -2, 0: 2 * odd - 3}

    load = pltpu.make_async_copy(orb_ref, slots.at[mine, :, :, :cells], load_sem.at[0])
    load.start()

    barrier = pltpu.get_barrier_semaphore()
    for by in (source[1], source[0]):
        pl.semaphore_signal(barrier, inc=1, device_id=at(by), device_id_type=MESH)
    pl.semaphore_signal(barrier, inc=1, device_id=sibling, device_id_type=MESH)
    for side in range(2):
        @pl.when(has[side])
        def _(side=side):
            for slot in (mine, 1, 0):
                pl.semaphore_signal(barrier, inc=1, device_id=at(source[slot], step_of[side]), device_id_type=MESH)

    lane = lax.broadcasted_iota(jnp.int32, (1, LANES), 1)
    low = lane < NZ
    column = lane % NZ

    def shuffle(a, b):
        turned = pltpu.roll(jnp.where(low, b, a), NZ, 1)
        return jnp.where(low, a, turned), jnp.where(low, turned, b)

    def z_next(value, by):
        return jnp.where(column < NZ - by, pltpu.roll(value, LANES - by, 1), 0.0)

    load.wait()
    for o in range(orbs):
        value = jnp.broadcast_to(occ_ref[:, o:o + 1].astype(jnp.float32), (planes, LANES))
        slots[mine, o, :, cells:] = value.astype(jnp.bfloat16)

    def rows_of(slot, o, k):
        return shuffle(slots[slot, o, :, lane_tile(k)].astype(jnp.float32),
                       slots[slot, o, :, lane_tile(k + half)].astype(jnp.float32))

    def cut(k):
        pairs = [rows_of(mine, o, k) for o in range(orbs)]
        for side in range(2):
            at_plane = 0 if side == 0 else planes - WIDTH
            parts = [pairs[o][h][at_plane:at_plane + WIDTH] for h in range(2) for o in range(orbs)]
            edges[side, k] = jnp.concatenate(parts, axis=0).astype(jnp.bfloat16)

    loop(half, cut, 2)

    for side in range(2):
        @pl.when(jnp.logical_not(has[side]))
        def _(side=side):
            halos[:, side] = jnp.zeros(halos.shape[:1] + halos.shape[2:], jnp.bfloat16)

    sides = has[0].astype(jnp.int32) + has[1].astype(jnp.int32)
    pl.semaphore_wait(barrier, 3 + 3 * sides)

    def edge_copy(side, slot):
        return pltpu.make_async_remote_copy(
            src_ref=edges.at[side], dst_ref=halos.at[slot, 1 - side],
            send_sem=edge_send.at[slot, side], recv_sem=edge_recv.at[slot, 1 - side],
            device_id=at(reach[slot], step_of[side]), device_id_type=MESH)

    def edge_pass(side):
        return pltpu.make_async_remote_copy(
            src_ref=halos.at[1, side], dst_ref=halos.at[2, side],
            send_sem=edge_send.at[2, side], recv_sem=edge_recv.at[2, side],
            device_id=sibling, device_id_type=MESH)

    def edge_wait(side, slot):
        pltpu.make_async_remote_copy(
            src_ref=edges.at[1 - side], dst_ref=halos.at[slot, side],
            send_sem=edge_send.at[slot, 1 - side], recv_sem=edge_recv.at[slot, side],
            device_id=sibling, device_id_type=MESH).wait_recv()

    def block_copy(slot, o):
        return pltpu.make_async_remote_copy(
            src_ref=slots.at[mine, o], dst_ref=slots.at[slot, o], send_sem=send_sem.at[slot, o],
            recv_sem=recv_sem.at[slot, o], device_id=at(reach[slot]), device_id_type=MESH)

    def block_pass(o):
        return pltpu.make_async_remote_copy(
            src_ref=slots.at[1, o], dst_ref=slots.at[2, o], send_sem=send_sem.at[2, o],
            recv_sem=recv_sem.at[2, o], device_id=sibling, device_id_type=MESH)

    def each_side(action):
        for side in range(2):
            pl.when(has[side])(functools.partial(action, side))

    each_side(lambda side: edge_copy(side, mine).start())
    each_side(lambda side: edge_copy(side, 1).start())
    each_side(lambda side: edge_copy(side, 0).start())
    for o in range(orbs):
        block_copy(1, o).start()
        block_copy(0, o).start()

    def prepare(t):
        row = lax.broadcasted_iota(jnp.int32, (planes, LANES), 0)
        lanes = lax.broadcasted_iota(jnp.int32, (planes, LANES), 1)
        col = lanes % NZ
        edge_z = jnp.logical_or(col == 0, col == NZ - 1)
        bottom = jnp.logical_and(t == 0, lanes < NZ)
        top = jnp.logical_and(t == tiles - 1, lanes >= NZ)
        first = jnp.logical_and(row == 0, jnp.logical_not(has[0]))
        last = jnp.logical_and(row == planes - 1, jnp.logical_not(has[1]))
        value = jnp.full((planes, LANES), outer + 6.0, jnp.float32)
        for walled in (edge_z, jnp.logical_or(bottom, top), first, last):
            value = value - jnp.where(walled, 1.0, 0.0)
        centre[t] = value

    loop(tiles, prepare)

    def seam(value, keep_low):
        return jnp.where(low if keep_low else jnp.logical_not(low), pltpu.roll(value, NZ, 1), 0.0)

    def widen(slot, dst):
        def body(k):
            borders = []
            for side in range(2):
                plain = halos[slot, side, k].astype(jnp.float32)
                borders.append((plain, z_next(plain, 1), z_next(plain, 2)))
            for o in range(orbs):
                for h, mid in enumerate(rows_of(slot, o, k)):
                    t = 2 * k + h + PAD
                    r = (h * orbs + o) * WIDTH
                    for which, value in enumerate((mid, z_next(mid, 1), z_next(mid, 2))):
                        dst[o, which, t, TOP:TOP + planes] = value
                        dst[o, which, t, TOP - WIDTH:TOP] = borders[0][which][r:r + WIDTH]
                        dst[o, which, t, TOP + planes:TOP + planes + WIDTH] = borders[1][which][r:r + WIDTH]
        loop(half, body, 2)
        rows = dst.shape[3]
        for o in range(orbs):
            for which in range(2):
                for n in range(PAD):
                    dst[o, which, n] = seam(dst[o, which, tiles + n], False)
                    dst[o, which, tiles + PAD + n] = seam(dst[o, which, PAD + n], True)

    start = TOP - WIDTH
    ext = wide.shape[2]

    def gather(slot, src, fresh):
        weights = [-scale * slots[slot, o, :, cells:].astype(jnp.float32) for o in range(orbs)]
        weights = [jnp.broadcast_to(w[:1], (ext, LANES)) for w in weights]

        def body(t):
            at_t = t + PAD
            w = [weights[o] * src[o, 0, at_t, start:start + ext] for o in range(orbs)]
            for n, (which, dx, dy) in enumerate(WIDE):
                value = None if fresh else wide[n, at_t]
                for o in range(orbs):
                    term = w[o] * src[o, which, at_t + dy, start + dx:start + dx + ext]
                    value = term if value is None else value + term
                wide[n, at_t] = value
            w = [w[o][WIDTH:WIDTH + planes] for o in range(orbs)] if False else [
                weights[o][:planes] * src[o, 0, at_t, TOP:TOP + planes] for o in range(orbs)]
            for n, (which, dy) in enumerate(FLAT):
                value = None if fresh else gram[n, at_t]
                for o in range(orbs):
                    term = w[o] * src[o, which, at_t + dy, TOP:TOP + planes]
                    value = term if value is None else value + term
                gram[n, at_t] = value
        loop(tiles, body, 2)

    def finish(t, i):
        at_t = t + PAD

        def orbital(which, dx=0, dy=0):
            return own[i, which, at_t + dy, TOP + dx:TOP + dx + planes]

        def flat(n, dy=0):
            return gram[n, at_t + dy]

        def deep(n, dx=0, dy=0):
            return wide[n, at_t + dy, WIDTH + dx:WIDTH + dx + planes]

        mid = orbital(0)
        near = orbital(0, 1) * deep(0) + orbital(0, -1) * deep(0, -1)
        near = near + (orbital(0, 0, 1) * flat(1) + orbital(0, 0, -1) * flat(1, -1))
        near = near + orbital(1) * flat(3)
        far = orbital(0, 2) * deep(1) + orbital(0, -2) * deep(1, -2)
        far = far + (orbital(0, 0, 2) * flat(2) + orbital(0, 0, -2) * flat(2, -2))
        far = far + orbital(2) * flat(4)
        diag = orbital(0, 1, 1) * deep(2) + orbital(0, -1, -1) * deep(2, -1, -1)
        diag = diag + (orbital(0, 1, -1) * deep(3) + orbital(0, -1, 1) * deep(3, -1, 1))
        diag = diag + (orbital(1, 1) * deep(4) + orbital(1, -1) * deep(5))
        diag = diag + (orbital(1, 0, 1) * flat(5) + orbital(1, 0, -1) * flat(6))
        back = orbital(0, -1) * deep(4, -1) + orbital(0, 1) * deep(5, 1)
        back = back + (orbital(0, 0, -1) * flat(5, -1) + orbital(0, 0, 1) * flat(6, 1))
        back = inner * (mid * flat(3)) + 2.0 * back
        far = far + pltpu.roll(mid * flat(4), 2, 1) + pltpu.roll(back, 1, 1)
        return centre[t] * (mid * flat(0)) + inner * near + (2.0 * diag + far)

    each_side(lambda side: edge_wait(side, mine))
    widen(mine, own)
    gather(mine, own, True)

    if_odd, if_even = (0, 1, 2), (1, 0, 2)

    def step(k):
        slot = jnp.int32(0)
        for n, (a, b) in enumerate(zip(if_odd, if_even)):
            slot = jnp.where(k == n, jnp.where(odd == 1, a, b), slot)
        for q in range(STEPS):
            @pl.when(slot == q)
            def _(q=q):
                each_side(lambda side: edge_wait(side, q))
                if q == 1:
                    each_side(lambda side: edge_pass(side).start())
                for p in range(orbs):
                    (block_pass(p) if q == 2 else block_copy(q, p)).wait_recv()
                    if q == 1:
                        block_pass(p).start()
        widen(slot, vis)
        gather(slot, vis, False)

    loop(len(if_odd), step)

    for n, (which, dy) in enumerate(FLAT):
        if dy > 0:
            for p in range(dy):
                gram[n, PAD - 1 - p] = seam(gram[n, PAD + tiles - 1 - p], False)
        if dy < 0:
            gram[n, PAD + tiles] = seam(gram[n, PAD], True)
    for n, (which, dx, dy) in enumerate(WIDE):
        if dy > 0:
            wide[n, PAD - 1] = seam(wide[n, PAD + tiles - 1], False)
        if dy < 0:
            wide[n, PAD + tiles] = seam(wide[n, PAD], True)

    def apply(k):
        for i in range(orbs):
            a, b = shuffle(finish(2 * k, i), finish(2 * k + 1, i))
            out_ref[i, :, lane_tile(k)] = a
            out_ref[i, :, lane_tile(k + half)] = b

    loop(half, apply)

    for o in range(orbs):
        block_copy(0, o).wait_send()
        block_copy(1, o).wait_send()
        block_pass(o).wait_send()
    for slot in (mine, 1, 0):
        each_side(lambda side: edge_copy(side, slot).wait_send())
    each_side(lambda side: edge_pass(side).wait_send())


def per_device(n_band, n_slab, orbitals, occupation):
    orbs, planes, cells = orbitals.shape
    tiles = cells // LANES
    ext = -(-(planes + 2 * WIDTH) // 8) * 8
    tall = planes + 2 * TOP
    occ = occupation.reshape(1, orbs)
    f32, bf16 = jnp.float32, jnp.bfloat16
    rows = 2 * orbs * WIDTH
    padded = tiles + 2 * PAD
    return pl.pallas_call(
        functools.partial(kernel, n_band, n_slab),
        out_shape=jax.ShapeDtypeStruct(orbitals.shape, f32),
        in_specs=[pl.BlockSpec(memory_space=pl.ANY), pl.BlockSpec(memory_space=pltpu.VMEM)],
        out_specs=pl.BlockSpec(memory_space=pltpu.VMEM),
        scratch_shapes=[
            pltpu.VMEM((STEPS + 1, orbs, planes, cells + LANES), bf16),
            pltpu.VMEM((2, tiles // 2, rows, LANES), bf16),
            pltpu.VMEM((STEPS + 1, 2, tiles // 2, rows, LANES), bf16),
            pltpu.VMEM((orbs, 3, padded, tall, LANES), f32),
            pltpu.VMEM((orbs, 3, padded, tall, LANES), f32),
            pltpu.VMEM((len(FLAT), padded, planes, LANES), f32),
            pltpu.VMEM((len(WIDE), padded, ext, LANES), f32),
            pltpu.VMEM((tiles, planes, LANES), f32),
            pltpu.SemaphoreType.DMA((1,)),
            pltpu.SemaphoreType.DMA((STEPS, orbs)),
            pltpu.SemaphoreType.DMA((STEPS, orbs)),
            pltpu.SemaphoreType.DMA((STEPS + 1, 2)),
            pltpu.SemaphoreType.DMA((STEPS + 1, 2)),
        ],
        compiler_params=pltpu.CompilerParams(collective_id=0, has_side_effects=True),
        name="exchange",
    )(orbitals, occ)


def solution(mesh):
    in_specs = (P("band", "slab", None), P("band"))
    out_specs = P("band", "slab", None)
    return jax.shard_map(
        functools.partial(per_device, mesh.shape["band"], mesh.shape["slab"]),
        mesh=mesh, in_specs=in_specs, out_specs=out_specs, check_vma=False,
    )
```

time: 26.4 us -> 29.3 us (1.11)
  Pallas kernels: 24.3 us -> 27.2 us
    pallas_call x1, Pallas kernels: 24.3 us -> 27.2 us  [per_device(): pl.pallas_call(functools.partial(kernel, n_band, n_slab), out_shape=jax.S...]
where the time goes in v1:
time: 29.3 us; the launch traced here: 29.1 us
  Pallas kernels  27.2 us (93%)
  local copies, waits for them, and re-layouts  1.87 us (6%)
    pallas_call x1, Pallas kernels, per_device(): pl.pallas_call(functools.partial(kernel, n_band, n_slab), out_shape=jax.S...  27.2 us
    unnamed x1, local copies, waits for them, and re-layouts  1.87 us

profile of v1, /device:TPU:0, one launch (start us, length us, event | category | flops | bytes accessed | tf_op | source)
XLA Modules:
  0.0 29.1 jit_solution(557034301527447100)
XLA Ops:
  0.0 27.2 %exchange.1 = f32[2,16,4096]{2,1,0:T(8,128)} custom-call(bf16[2,16,4096]{2,1,0:T(8,128)(2,1)} %orb_ref.1, bf16[1,2]{1,0:T(2,128)(2,1)} %bitcast.1), custom_call_target="tpu_custom_call" | custom-call | tf_op jit(solution)/shard_map/exchange/pallas_call | solution.py:309
  27.3 1.9 %copy.4 = f32[2,16,4096]{2,1,0:T(8,128)} copy(f32[2,16,4096]{2,1,0:T(8,128)} %exchange.1) | data formatting | bytes 1048576

commit v2 on v1

--- a/solution.py
+++ b/solution.py
@@ -13,6 +13,7 @@
 LANES = 128
 WIDTH = 2
 PAD = 2
+GROUP = 4
 TOP = 8
 FLAT = ((0, 0), (0, 1), (0, 2), (1, 0), (2, 0), (1, 1), (1, -1))
 WIDE = ((0, 1, 0), (0, 2, 0), (0, 1, 1), (0, 1, -1), (1, 1, 0), (1, -1, 0))
@@ -41,7 +42,7 @@
 
 
 def kernel(n_band, n_slab, orb_ref, occ_ref, out_ref, slots, edges, halos, own, vis, gram, wide, centre,
-           load_sem, send_sem, recv_sem, edge_send, edge_recv):
+           moves, rest, load_sem, send_sem, recv_sem, edge_send, edge_recv):
     orbs, planes, cells = orb_ref.shape
     tiles = cells // LANES
     half = tiles // 2
@@ -79,26 +80,23 @@
         turned = pltpu.roll(jnp.where(low, b, a), NZ, 1)
         return jnp.where(low, a, turned), jnp.where(low, turned, b)
 
-    def z_next(value, by):
-        return jnp.where(column < NZ - by, pltpu.roll(value, LANES - by, 1), 0.0)
-
     load.wait()
     for o in range(orbs):
         value = jnp.broadcast_to(occ_ref[:, o:o + 1].astype(jnp.float32), (planes, LANES))
         slots[mine, o, :, cells:] = value.astype(jnp.bfloat16)
 
-    def rows_of(slot, o, k):
-        return shuffle(slots[slot, o, :, lane_tile(k)].astype(jnp.float32),
-                       slots[slot, o, :, lane_tile(k + half)].astype(jnp.float32))
-
-    def cut(k):
-        pairs = [rows_of(mine, o, k) for o in range(orbs)]
+    def cut(g):
+        parts = ([], [])
+        for n in range(GROUP):
+            for o in range(orbs):
+                pair = [slots[mine, o, :, lane_tile(GROUP * g + n + part * half)].astype(jnp.float32) for part in range(2)]
+                for side in range(2):
+                    at_plane = 0 if side == 0 else planes - WIDTH
+                    parts[side].append(jnp.concatenate([p[at_plane:at_plane + WIDTH] for p in pair], axis=1))
         for side in range(2):
-            at_plane = 0 if side == 0 else planes - WIDTH
-            parts = [pairs[o][h][at_plane:at_plane + WIDTH] for h in range(2) for o in range(orbs)]
-            edges[side, k] = jnp.concatenate(parts, axis=0).astype(jnp.bfloat16)
-
-    loop(half, cut, 2)
+            edges[side, g] = jnp.concatenate(parts[side], axis=0).astype(jnp.bfloat16)
+
+    loop(half // GROUP, cut)
 
     for side in range(2):
         @pl.when(jnp.logical_not(has[side]))
@@ -163,25 +161,38 @@
 
     loop(tiles, prepare)
 
+    source_lane = lax.broadcasted_iota(jnp.int32, (2 * LANES, LANES), 0)
+    target_lane = lax.broadcasted_iota(jnp.int32, (2 * LANES, LANES), 1)
+    for which in range(3):
+        for h in range(2):
+            wanted = (target_lane // NZ) * LANES + h * NZ + target_lane % NZ + which
+            hit = jnp.logical_and(source_lane == wanted, target_lane % NZ + which < NZ)
+            c = (2 * which + h) * LANES
+            moves[:, c:c + LANES] = jnp.where(hit, 1.0, 0.0).astype(jnp.bfloat16)
+
     def seam(value, keep_low):
         return jnp.where(low if keep_low else jnp.logical_not(low), pltpu.roll(value, NZ, 1), 0.0)
 
     def widen(slot, dst):
-        def body(k):
-            borders = []
-            for side in range(2):
-                plain = halos[slot, side, k].astype(jnp.float32)
-                borders.append((plain, z_next(plain, 1), z_next(plain, 2)))
-            for o in range(orbs):
-                for h, mid in enumerate(rows_of(slot, o, k)):
-                    t = 2 * k + h + PAD
-                    r = (h * orbs + o) * WIDTH
-                    for which, value in enumerate((mid, z_next(mid, 1), z_next(mid, 2))):
-                        dst[o, which, t, TOP:TOP + planes] = value
-                        dst[o, which, t, TOP - WIDTH:TOP] = borders[0][which][r:r + WIDTH]
-                        dst[o, which, t, TOP + planes:TOP + planes + WIDTH] = borders[1][which][r:r + WIDTH]
-        loop(half, body, 2)
-        rows = dst.shape[3]
+        matrix = moves[...]
+        for o in range(orbs):
+            stacked = jnp.concatenate(
+                [jnp.concatenate([slots[slot, o, :, (k + part * half) * LANES:(k + part * half + 1) * LANES]
+                                  for part in range(2)], axis=1) for k in range(half)], axis=0)
+            moved = jnp.dot(stacked, matrix, preferred_element_type=jnp.float32)
+            for k in range(half):
+                for n in range(6):
+                    dst[o, n // 2, 2 * k + n % 2 + PAD, TOP:TOP + planes] = moved[
+                        k * planes:(k + 1) * planes, n * LANES:(n + 1) * LANES]
+        for side in range(2):
+            stacked = jnp.concatenate([halos[slot, side, g] for g in range(half // GROUP)], axis=0)
+            moved = jnp.dot(stacked, matrix[:, :4 * LANES], preferred_element_type=jnp.float32)
+            to = TOP - WIDTH if side == 0 else TOP + planes
+            for k in range(half):
+                for o in range(orbs):
+                    r = (k * orbs + o) * WIDTH
+                    for n in range(4):
+                        dst[o, n // 2, 2 * k + n % 2 + PAD, to:to + WIDTH] = moved[r:r + WIDTH, n * LANES:(n + 1) * LANES]
         for o in range(orbs):
             for which in range(2):
                 for n in range(PAD):
@@ -204,8 +215,7 @@
                     term = w[o] * src[o, which, at_t + dy, start + dx:start + dx + ext]
                     value = term if value is None else value + term
                 wide[n, at_t] = value
-            w = [w[o][WIDTH:WIDTH + planes] for o in range(orbs)] if False else [
-                weights[o][:planes] * src[o, 0, at_t, TOP:TOP + planes] for o in range(orbs)]
+            w = [weights[o][:planes] * src[o, 0, at_t, TOP:TOP + planes] for o in range(orbs)]
             for n, (which, dy) in enumerate(FLAT):
                 value = None if fresh else gram[n, at_t]
                 for o in range(orbs):
@@ -240,8 +250,9 @@
         back = orbital(0, -1) * deep(4, -1) + orbital(0, 1) * deep(5, 1)
         back = back + (orbital(0, 0, -1) * flat(5, -1) + orbital(0, 0, 1) * flat(6, 1))
         back = inner * (mid * flat(3)) + 2.0 * back
-        far = far + pltpu.roll(mid * flat(4), 2, 1) + pltpu.roll(back, 1, 1)
-        return centre[t] * (mid * flat(0)) + inner * near + (2.0 * diag + far)
+        rest[0, i, t] = centre[t] * (mid * flat(0)) + inner * near + (2.0 * diag + far)
+        rest[1, i, t] = back
+        rest[2, i, t] = mid * flat(4)
 
     each_side(lambda side: edge_wait(side, mine))
     widen(mine, own)
@@ -280,13 +291,22 @@
         if dy < 0:
             wide[n, PAD + tiles] = seam(wide[n, PAD], True)
 
+    def products(t):
+        for i in range(orbs):
+            finish(t, i)
+
+    loop(tiles, products)
+
+    def total(t, i):
+        return rest[0, i, t] + pltpu.roll(rest[1, i, t], 1, 1) + pltpu.roll(rest[2, i, t], 2, 1)
+
     def apply(k):
         for i in range(orbs):
-            a, b = shuffle(finish(2 * k, i), finish(2 * k + 1, i))
+            a, b = shuffle(total(2 * k, i), total(2 * k + 1, i))
             out_ref[i, :, lane_tile(k)] = a
             out_ref[i, :, lane_tile(k + half)] = b
 
-    loop(half, apply)
+    loop(half, apply, 8)
 
     for o in range(orbs):
         block_copy(0, o).wait_send()
@@ -304,22 +324,24 @@
     tall = planes + 2 * TOP
     occ = occupation.reshape(1, orbs)
     f32, bf16 = jnp.float32, jnp.bfloat16
-    rows = 2 * orbs * WIDTH
+    rows, groups = GROUP * orbs * WIDTH, tiles // (2 * GROUP)
     padded = tiles + 2 * PAD
     return pl.pallas_call(
         functools.partial(kernel, n_band, n_slab),
-        out_shape=jax.ShapeDtypeStruct(orbitals.shape, f32),
+        out_shape=pltpu.VMEM(orbitals.shape, f32),
         in_specs=[pl.BlockSpec(memory_space=pl.ANY), pl.BlockSpec(memory_space=pltpu.VMEM)],
         out_specs=pl.BlockSpec(memory_space=pltpu.VMEM),
         scratch_shapes=[
             pltpu.VMEM((STEPS + 1, orbs, planes, cells + LANES), bf16),
-            pltpu.VMEM((2, tiles // 2, rows, LANES), bf16),
-            pltpu.VMEM((STEPS + 1, 2, tiles // 2, rows, LANES), bf16),
+            pltpu.VMEM((2, groups, rows, 2 * LANES), bf16),
+            pltpu.VMEM((STEPS + 1, 2, groups, rows, 2 * LANES), bf16),
             pltpu.VMEM((orbs, 3, padded, tall, LANES), f32),
             pltpu.VMEM((orbs, 3, padded, tall, LANES), f32),
             pltpu.VMEM((len(FLAT), padded, planes, LANES), f32),
             pltpu.VMEM((len(WIDE), padded, ext, LANES), f32),
             pltpu.VMEM((tiles, planes, LANES), f32),
+            pltpu.VMEM((2 * LANES, 6 * LANES), bf16),
+            pltpu.VMEM((3, orbs, tiles, planes, LANES), f32),
             pltpu.SemaphoreType.DMA((1,)),
             pltpu.SemaphoreType.DMA((STEPS, orbs)),
             pltpu.SemaphoreType.DMA((STEPS, orbs)),

time: 29.3 us -> 24.4 us (0.83)
  Pallas kernels: 27.2 us -> 23.4 us
  local copies, waits for them, and re-layouts: 1.87 us -> 0.8 us
    pallas_call x1, Pallas kernels: 27.2 us -> 23.4 us  [per_device(): pl.pallas_call(functools.partial(kernel, n_band, n_slab), out_shape=pltpu...]
    unnamed x1, local copies, waits for them, and re-layouts: 1.87 us -> 0.8 us
where the time goes in v2:
time: 24.4 us; the launch traced here: 24.2 us
  Pallas kernels  23.4 us (96%)
  local copies, waits for them, and re-layouts  0.8 us (3%)
    pallas_call x1, Pallas kernels, per_device(): pl.pallas_call(functools.partial(kernel, n_band, n_slab), out_shape=pltpu...  23.4 us
    unnamed x1, local copies, waits for them, and re-layouts  0.8 us

profile of v2, /device:TPU:0, one launch (start us, length us, event | category | flops | bytes accessed | tf_op | source)
XLA Modules:
  0.0 24.2 jit_solution(4184458260937865987)
XLA Ops:
  0.0 23.4 %exchange.1 = f32[2,16,4096]{2,1,0:T(8,128)S(1)} custom-call(bf16[2,16,4096]{2,1,0:T(8,128)(2,1)} %orb_ref.1, bf16[1,2]{1,0:T(2,128)(2,1)} %bitcast.1), custom_call_target="tpu_custom_call" | custom-call | tf_op jit(solution)/shard_map/exchange/pallas_call | solution.py:329
  23.4 0.8 %copy.4 = f32[2,16,4096]{2,1,0:T(8,128)} copy(f32[2,16,4096]{2,1,0:T(8,128)S(1)} %exchange.1) | data formatting | bytes 1048576

commit v3 on v2

--- a/solution.py
+++ b/solution.py
@@ -14,6 +14,8 @@
 WIDTH = 2
 PAD = 2
 GROUP = 4
+CHUNKS = 4
+SENDS = STEPS + 2
 TOP = 8
 FLAT = ((0, 0), (0, 1), (0, 2), (1, 0), (2, 0), (1, 1), (1, -1))
 WIDE = ((0, 1, 0), (0, 2, 0), (0, 1, 1), (0, 1, -1), (1, 1, 0), (1, -1, 0))
@@ -46,31 +48,49 @@
     orbs, planes, cells = orb_ref.shape
     tiles = cells // LANES
     half = tiles // 2
-    mine = STEPS
+    groups = half // GROUP
+    mine, carry = 0, STEPS + 1
+    chunk = half * LANES // CHUNKS
     band, slab = lax.axis_index("band"), lax.axis_index("slab")
-    odd = lax.rem(band, 2)
+    kind = lax.rem(band, 4)
+    is_d = kind == 3
+
+    def by_kind(a, b, c, d):
+        return jnp.where(kind == 0, a, jnp.where(kind == 1, b, jnp.where(kind == 2, c, d)))
 
     def at(by, side=0):
         return {"band": lax.rem(band + by + n_band, n_band), "slab": slab + side}
 
-    sibling = at(1 - 2 * odd)
+    sibling = at(by_kind(1, -1, 1, -1))
     has = (slab > 0, slab < n_slab - 1)
     step_of = (-1, 1)
-    reach = {mine: 0, 1: 2, 0: 1 + 2 * odd}
-    source = {mine: 0, 1: -2, 0: 2 * odd - 3}
-
-    load = pltpu.make_async_copy(orb_ref, slots.at[mine, :, :, :cells], load_sem.at[0])
-    load.start()
+    slot_x, reach_x = by_kind(2, 2, 2, carry), by_kind(2, 2, 2, 4)
+    slot_y, reach_y = by_kind(1, 3, 1, 1), by_kind(1, 3, 1, 1)
+    slot_pass = by_kind(3, 1, 3, 1)
+
+    loads = [pltpu.make_async_copy(orb_ref.at[:, :, part * half * LANES:(part + 1) * half * LANES],
+                                   slots.at[mine, :, part], load_sem.at[part]) for part in range(2)]
+    for load in loads:
+        load.start()
 
     barrier = pltpu.get_barrier_semaphore()
-    for by in (source[1], source[0]):
-        pl.semaphore_signal(barrier, inc=1, device_id=at(by), device_id_type=MESH)
-    pl.semaphore_signal(barrier, inc=1, device_id=sibling, device_id_type=MESH)
-    for side in range(2):
-        @pl.when(has[side])
-        def _(side=side):
-            for slot in (mine, 1, 0):
-                pl.semaphore_signal(barrier, inc=1, device_id=at(source[slot], step_of[side]), device_id_type=MESH)
+    sides = has[0].astype(jnp.int32) + has[1].astype(jnp.int32)
+    straight = {0: (1, -2, -3), 1: (-1, 2), 2: (-2, 1), 3: (-1, -2, -4)}
+    slanted = {0: (-2, -3), 1: (-1,), 2: (-2,), 3: (-1, -2, -4)}
+
+    def greet(by, side=0):
+        pl.semaphore_signal(barrier, inc=1, device_id=at(by, side), device_id_type=MESH)
+
+    for which in range(4):
+        @pl.when(kind == which)
+        def _(which=which):
+            for by in sorted(straight[which]):
+                greet(by)
+            for side in range(2):
+                @pl.when(has[side])
+                def _(side=side):
+                    for by in sorted(slanted[which]) + [0]:
+                        greet(by, step_of[side])
 
     lane = lax.broadcasted_iota(jnp.int32, (1, LANES), 1)
     low = lane < NZ
@@ -80,70 +100,87 @@
         turned = pltpu.roll(jnp.where(low, b, a), NZ, 1)
         return jnp.where(low, a, turned), jnp.where(low, turned, b)
 
-    load.wait()
-    for o in range(orbs):
-        value = jnp.broadcast_to(occ_ref[:, o:o + 1].astype(jnp.float32), (planes, LANES))
-        slots[mine, o, :, cells:] = value.astype(jnp.bfloat16)
+    for load in loads:
+        load.wait()
+    for side in range(2):
+        rows = [jnp.broadcast_to(occ_ref[:, o:o + 1].astype(jnp.float32), (1, 2 * LANES)) for o in range(orbs)]
+        rows.append(jnp.zeros((edges.shape[2] - orbs, 2 * LANES), jnp.float32))
+        edges[side, groups] = jnp.concatenate(rows, axis=0).astype(jnp.bfloat16)
 
     def cut(g):
         parts = ([], [])
         for n in range(GROUP):
             for o in range(orbs):
-                pair = [slots[mine, o, :, lane_tile(GROUP * g + n + part * half)].astype(jnp.float32) for part in range(2)]
+                pair = [slots[mine, o, part, :, lane_tile(GROUP * g + n)].astype(jnp.float32) for part in range(2)]
                 for side in range(2):
                     at_plane = 0 if side == 0 else planes - WIDTH
                     parts[side].append(jnp.concatenate([p[at_plane:at_plane + WIDTH] for p in pair], axis=1))
         for side in range(2):
             edges[side, g] = jnp.concatenate(parts[side], axis=0).astype(jnp.bfloat16)
 
-    loop(half // GROUP, cut)
+    loop(groups, cut)
 
     for side in range(2):
         @pl.when(jnp.logical_not(has[side]))
         def _(side=side):
             halos[:, side] = jnp.zeros(halos.shape[:1] + halos.shape[2:], jnp.bfloat16)
 
-    sides = has[0].astype(jnp.int32) + has[1].astype(jnp.int32)
-    pl.semaphore_wait(barrier, 3 + 3 * sides)
-
-    def edge_copy(side, slot):
+    pl.semaphore_wait(barrier, by_kind(2, 3, 2, 3) + sides * by_kind(3, 3, 3, 2))
+
+    def edge_copy(side, slot, by):
         return pltpu.make_async_remote_copy(
             src_ref=edges.at[side], dst_ref=halos.at[slot, 1 - side],
             send_sem=edge_send.at[slot, side], recv_sem=edge_recv.at[slot, 1 - side],
-            device_id=at(reach[slot], step_of[side]), device_id_type=MESH)
-
-    def edge_pass(side):
+            device_id=at(by, step_of[side]), device_id_type=MESH)
+
+    def edge_pass(side, src, slot, device, sem):
         return pltpu.make_async_remote_copy(
-            src_ref=halos.at[1, side], dst_ref=halos.at[2, side],
-            send_sem=edge_send.at[2, side], recv_sem=edge_recv.at[2, side],
-            device_id=sibling, device_id_type=MESH)
-
-    def edge_wait(side, slot):
-        pltpu.make_async_remote_copy(
-            src_ref=edges.at[1 - side], dst_ref=halos.at[slot, side],
-            send_sem=edge_send.at[slot, 1 - side], recv_sem=edge_recv.at[slot, side],
-            device_id=sibling, device_id_type=MESH).wait_recv()
-
-    def block_copy(slot, o):
+            src_ref=halos.at[src, side], dst_ref=halos.at[slot, side],
+            send_sem=edge_send.at[sem, side], recv_sem=edge_recv.at[slot, side],
+            device_id=device, device_id_type=MESH)
+
+    def piece(ref, slot, c):
+        return ref.at[slot, :, :, :, c * chunk:(c + 1) * chunk]
+
+    def block_copy(src, slot, c, device, sem):
         return pltpu.make_async_remote_copy(
-            src_ref=slots.at[mine, o], dst_ref=slots.at[slot, o], send_sem=send_sem.at[slot, o],
-            recv_sem=recv_sem.at[slot, o], device_id=at(reach[slot]), device_id_type=MESH)
-
-    def block_pass(o):
-        return pltpu.make_async_remote_copy(
-            src_ref=slots.at[1, o], dst_ref=slots.at[2, o], send_sem=send_sem.at[2, o],
-            recv_sem=recv_sem.at[2, o], device_id=sibling, device_id_type=MESH)
+            src_ref=piece(slots, src, c), dst_ref=piece(slots, slot, c), send_sem=send_sem.at[sem, c],
+            recv_sem=recv_sem.at[slot, c], device_id=device, device_id_type=MESH)
 
     def each_side(action):
         for side in range(2):
             pl.when(has[side])(functools.partial(action, side))
 
-    each_side(lambda side: edge_copy(side, mine).start())
-    each_side(lambda side: edge_copy(side, 1).start())
-    each_side(lambda side: edge_copy(side, 0).start())
-    for o in range(orbs):
-        block_copy(1, o).start()
-        block_copy(0, o).start()
+    def send_x(c):
+        return block_copy(mine, slot_x, c, at(reach_x), 0)
+
+    def send_y(c):
+        return block_copy(mine, slot_y, c, at(reach_y), 1)
+
+    def send_on(c):
+        return block_copy(2, slot_pass, c, sibling, 2)
+
+    def relays(c):
+        return (block_copy(carry, 2, c, at(-2), 3), block_copy(carry, 3, c, at(-1), 4))
+
+    def edge_on(side):
+        return edge_pass(side, 2, slot_pass, sibling, SENDS)
+
+    def edge_relays(side):
+        return (edge_pass(side, carry, 2, at(-2), SENDS + 1), edge_pass(side, carry, 3, at(-1), SENDS + 2))
+
+    def arrived(slot, c):
+        block_copy(mine, slot, c, sibling, 0).wait_recv()
+
+    def edge_arrived(slot):
+        each_side(lambda side: edge_pass(side, mine, slot, sibling, 0).wait_recv())
+
+    each_side(lambda side: edge_copy(side, mine, 0).start())
+    each_side(lambda side: edge_copy(side, slot_x, reach_x).start())
+    pl.when(jnp.logical_not(is_d))(lambda: each_side(lambda side: edge_copy(side, slot_y, reach_y).start()))
+    for c in range(CHUNKS):
+        send_x(c).start()
+        pl.when(jnp.logical_not(is_d))(lambda c=c: send_y(c).start())
 
     def prepare(t):
         row = lax.broadcasted_iota(jnp.int32, (planes, LANES), 0)
@@ -177,7 +214,7 @@
         matrix = moves[...]
         for o in range(orbs):
             stacked = jnp.concatenate(
-                [jnp.concatenate([slots[slot, o, :, (k + part * half) * LANES:(k + part * half + 1) * LANES]
+                [jnp.concatenate([slots[slot, o, part, :, k * LANES:(k + 1) * LANES]
                                   for part in range(2)], axis=1) for k in range(half)], axis=0)
             moved = jnp.dot(stacked, matrix, preferred_element_type=jnp.float32)
             for k in range(half):
@@ -185,7 +222,7 @@
                     dst[o, n // 2, 2 * k + n % 2 + PAD, TOP:TOP + planes] = moved[
                         k * planes:(k + 1) * planes, n * LANES:(n + 1) * LANES]
         for side in range(2):
-            stacked = jnp.concatenate([halos[slot, side, g] for g in range(half // GROUP)], axis=0)
+            stacked = jnp.concatenate([halos[slot, side, g] for g in range(groups)], axis=0)
             moved = jnp.dot(stacked, matrix[:, :4 * LANES], preferred_element_type=jnp.float32)
             to = TOP - WIDTH if side == 0 else TOP + planes
             for k in range(half):
@@ -203,8 +240,12 @@
     ext = wide.shape[2]
 
     def gather(slot, src, fresh):
-        weights = [-scale * slots[slot, o, :, cells:].astype(jnp.float32) for o in range(orbs)]
-        weights = [jnp.broadcast_to(w[:1], (ext, LANES)) for w in weights]
+        if fresh:
+            rows = edges[0, groups]
+        else:
+            rows = jnp.where(has[0], halos[slot, 0, groups].astype(jnp.float32), halos[slot, 1, groups].astype(jnp.float32))
+        rows = -scale * rows[:orbs, :LANES].astype(jnp.float32)
+        weights = [jnp.broadcast_to(rows[o:o + 1], (ext, LANES)) for o in range(orbs)]
 
         def body(t):
             at_t = t + PAD
@@ -254,30 +295,48 @@
         rest[1, i, t] = back
         rest[2, i, t] = mid * flat(4)
 
-    each_side(lambda side: edge_wait(side, mine))
+    edge_arrived(mine)
     widen(mine, own)
     gather(mine, own, True)
 
-    if_odd, if_even = (0, 1, 2), (1, 0, 2)
-
-    def step(k):
-        slot = jnp.int32(0)
-        for n, (a, b) in enumerate(zip(if_odd, if_even)):
-            slot = jnp.where(k == n, jnp.where(odd == 1, a, b), slot)
-        for q in range(STEPS):
-            @pl.when(slot == q)
-            def _(q=q):
-                each_side(lambda side: edge_wait(side, q))
-                if q == 1:
-                    each_side(lambda side: edge_pass(side).start())
-                for p in range(orbs):
-                    (block_pass(p) if q == 2 else block_copy(q, p)).wait_recv()
-                    if q == 1:
-                        block_pass(p).start()
+    def step(n):
+        slot = jnp.where(n == 0, by_kind(3, 1, 2, 1), jnp.where(n == 1, by_kind(2, 2, 1, 2), by_kind(1, 3, 3, 3)))
+
+        @pl.when(slot == 2)
+        def _():
+            edge_arrived(2)
+            each_side(lambda side: edge_on(side).start())
+
+            @pl.when(is_d)
+            def _():
+                edge_arrived(carry)
+
+                def hand_on(side):
+                    for copy in edge_relays(side):
+                        copy.start()
+
+                each_side(hand_on)
+
+            for c in range(CHUNKS):
+                arrived(2, c)
+                send_on(c).start()
+
+                @pl.when(is_d)
+                def _(c=c):
+                    arrived(carry, c)
+                    for copy in relays(c):
+                        copy.start()
+
+        @pl.when(slot != 2)
+        def _():
+            edge_arrived(slot)
+            for c in range(CHUNKS):
+                arrived(slot, c)
+
         widen(slot, vis)
         gather(slot, vis, False)
 
-    loop(len(if_odd), step)
+    loop(STEPS, step)
 
     for n, (which, dy) in enumerate(FLAT):
         if dy > 0:
@@ -308,13 +367,29 @@
 
     loop(half, apply, 8)
 
-    for o in range(orbs):
-        block_copy(0, o).wait_send()
-        block_copy(1, o).wait_send()
-        block_pass(o).wait_send()
-    for slot in (mine, 1, 0):
-        each_side(lambda side: edge_copy(side, slot).wait_send())
-    each_side(lambda side: edge_pass(side).wait_send())
+    each_side(lambda side: edge_copy(side, mine, 0).wait_send())
+    each_side(lambda side: edge_copy(side, slot_x, reach_x).wait_send())
+    each_side(lambda side: edge_on(side).wait_send())
+    for c in range(CHUNKS):
+        send_x(c).wait_send()
+        send_on(c).wait_send()
+
+    @pl.when(jnp.logical_not(is_d))
+    def _():
+        each_side(lambda side: edge_copy(side, slot_y, reach_y).wait_send())
+        for c in range(CHUNKS):
+            send_y(c).wait_send()
+
+    @pl.when(is_d)
+    def _():
+        def sent(side):
+            for copy in edge_relays(side):
+                copy.wait_send()
+
+        each_side(sent)
+        for c in range(CHUNKS):
+            for copy in relays(c):
+                copy.wait_send()
 
 
 def per_device(n_band, n_slab, orbitals, occupation):
@@ -332,9 +407,9 @@
         in_specs=[pl.BlockSpec(memory_space=pl.ANY), pl.BlockSpec(memory_space=pltpu.VMEM)],
         out_specs=pl.BlockSpec(memory_space=pltpu.VMEM),
         scratch_shapes=[
-            pltpu.VMEM((STEPS + 1, orbs, planes, cells + LANES), bf16),
-            pltpu.VMEM((2, groups, rows, 2 * LANES), bf16),
-            pltpu.VMEM((STEPS + 1, 2, groups, rows, 2 * LANES), bf16),
+            pltpu.VMEM((SENDS, orbs, 2, planes, cells // 2), bf16),
+            pltpu.VMEM((2, groups + 1, rows, 2 * LANES), bf16),
+            pltpu.VMEM((SENDS, 2, groups + 1, rows, 2 * LANES), bf16),
             pltpu.VMEM((orbs, 3, padded, tall, LANES), f32),
             pltpu.VMEM((orbs, 3, padded, tall, LANES), f32),
             pltpu.VMEM((len(FLAT), padded, planes, LANES), f32),
@@ -342,11 +417,11 @@
             pltpu.VMEM((tiles, planes, LANES), f32),
             pltpu.VMEM((2 * LANES, 6 * LANES), bf16),
             pltpu.VMEM((3, orbs, tiles, planes, LANES), f32),
-            pltpu.SemaphoreType.DMA((1,)),
-            pltpu.SemaphoreType.DMA((STEPS, orbs)),
-            pltpu.SemaphoreType.DMA((STEPS, orbs)),
-            pltpu.SemaphoreType.DMA((STEPS + 1, 2)),
-            pltpu.SemaphoreType.DMA((STEPS + 1, 2)),
+            pltpu.SemaphoreType.DMA((2,)),
+            pltpu.SemaphoreType.DMA((SENDS, CHUNKS)),
+            pltpu.SemaphoreType.DMA((SENDS, CHUNKS)),
+            pltpu.SemaphoreType.DMA((SENDS + 3, 2)),
+            pltpu.SemaphoreType.DMA((SENDS, 2)),
         ],
         compiler_params=pltpu.CompilerParams(collective_id=0, has_side_effects=True),
         name="exchange",

time: 24.4 us -> 23.2 us (0.951)
  Pallas kernels: 23.4 us -> 22.2 us
    pallas_call x1, Pallas kernels: 23.4 us -> 22.2 us  [per_device(): pl.pallas_call(functools.partial(kernel, n_band, n_slab), out_shape=pltpu...]
where the time goes in v3:
time: 23.2 us; the launch traced here: 23 us
  Pallas kernels  22.2 us (96%)
  local copies, waits for them, and re-layouts  0.8 us (3%)
    pallas_call x1, Pallas kernels, per_device(): pl.pallas_call(functools.partial(kernel, n_band, n_slab), out_shape=pltpu...  22.2 us
    unnamed x1, local copies, waits for them, and re-layouts  0.8 us

profile of v3, /device:TPU:0, one launch (start us, length us, event | category | flops | bytes accessed | tf_op | source)
XLA Modules:
  0.0 23.0 jit_solution(10361591718568953358)
XLA Ops:
  0.0 22.2 %exchange.1 = f32[2,16,4096]{2,1,0:T(8,128)S(1)} custom-call(bf16[2,16,4096]{2,1,0:T(8,128)(2,1)} %orb_ref.1, bf16[1,2]{1,0:T(2,128)(2,1)} %bitcast.1), custom_call_target="tpu_custom_call" | custom-call | tf_op jit(solution)/shard_map/exchange/pallas_call | solution.py:404
  22.2 0.8 %copy.4 = f32[2,16,4096]{2,1,0:T(8,128)} copy(f32[2,16,4096]{2,1,0:T(8,128)S(1)} %exchange.1) | data formatting | bytes 1048576

commit v4 on v3

--- a/solution.py
+++ b/solution.py
@@ -15,7 +15,7 @@
 PAD = 2
 GROUP = 4
 CHUNKS = 4
-SENDS = STEPS + 2
+SENDS = STEPS + 1
 TOP = 8
 FLAT = ((0, 0), (0, 1), (0, 2), (1, 0), (2, 0), (1, 1), (1, -1))
 WIDE = ((0, 1, 0), (0, 2, 0), (0, 1, 1), (0, 1, -1), (1, 1, 0), (1, -1, 0))
@@ -44,16 +44,16 @@
 
 
 def kernel(n_band, n_slab, orb_ref, occ_ref, out_ref, slots, edges, halos, own, vis, gram, wide, centre,
-           moves, rest, load_sem, send_sem, recv_sem, edge_send, edge_recv):
+           moves, rest, occ, load_sem, send_sem, recv_sem, edge_send, edge_recv):
     orbs, planes, cells = orb_ref.shape
     tiles = cells // LANES
     half = tiles // 2
     groups = half // GROUP
-    mine, carry = 0, STEPS + 1
+    mine = 0
     chunk = half * LANES // CHUNKS
     band, slab = lax.axis_index("band"), lax.axis_index("slab")
     kind = lax.rem(band, 4)
-    is_d = kind == 3
+    is_b, is_d = kind == 1, kind == 3
 
     def by_kind(a, b, c, d):
         return jnp.where(kind == 0, a, jnp.where(kind == 1, b, jnp.where(kind == 2, c, d)))
@@ -64,19 +64,19 @@
     sibling = at(by_kind(1, -1, 1, -1))
     has = (slab > 0, slab < n_slab - 1)
     step_of = (-1, 1)
-    slot_x, reach_x = by_kind(2, 2, 2, carry), by_kind(2, 2, 2, 4)
-    slot_y, reach_y = by_kind(1, 3, 1, 1), by_kind(1, 3, 1, 1)
+    reach_y, slot_y = by_kind(1, 3, 1, 1), by_kind(1, 3, 1, 1)
     slot_pass = by_kind(3, 1, 3, 1)
 
     loads = [pltpu.make_async_copy(orb_ref.at[:, :, part * half * LANES:(part + 1) * half * LANES],
                                    slots.at[mine, :, part], load_sem.at[part]) for part in range(2)]
+    loads.append(pltpu.make_async_copy(occ_ref, occ, load_sem.at[2]))
     for load in loads:
         load.start()
 
     barrier = pltpu.get_barrier_semaphore()
     sides = has[0].astype(jnp.int32) + has[1].astype(jnp.int32)
-    straight = {0: (1, -2, -3), 1: (-1, 2), 2: (-2, 1), 3: (-1, -2, -4)}
-    slanted = {0: (-2, -3), 1: (-1,), 2: (-2,), 3: (-1, -2, -4)}
+    straight = {0: (1, -2, -3), 1: (-1, -2), 2: (-2, 1, -1), 3: (-1, -2)}
+    slanted = {0: (-2, -3), 1: (-1, -2), 2: (-2,), 3: (-1, -2)}
 
     def greet(by, side=0):
         pl.semaphore_signal(barrier, inc=1, device_id=at(by, side), device_id_type=MESH)
@@ -103,7 +103,7 @@
     for load in loads:
         load.wait()
     for side in range(2):
-        rows = [jnp.broadcast_to(occ_ref[:, o:o + 1].astype(jnp.float32), (1, 2 * LANES)) for o in range(orbs)]
+        rows = [jnp.broadcast_to(occ[:, o:o + 1].astype(jnp.float32), (1, 2 * LANES)) for o in range(orbs)]
         rows.append(jnp.zeros((edges.shape[2] - orbs, 2 * LANES), jnp.float32))
         edges[side, groups] = jnp.concatenate(rows, axis=0).astype(jnp.bfloat16)
 
@@ -125,7 +125,7 @@
         def _(side=side):
             halos[:, side] = jnp.zeros(halos.shape[:1] + halos.shape[2:], jnp.bfloat16)
 
-    pl.semaphore_wait(barrier, by_kind(2, 3, 2, 3) + sides * by_kind(3, 3, 3, 2))
+    pl.semaphore_wait(barrier, by_kind(2, 4, 2, 2) + sides * by_kind(3, 3, 3, 2))
 
     def edge_copy(side, slot, by):
         return pltpu.make_async_remote_copy(
@@ -152,7 +152,7 @@
             pl.when(has[side])(functools.partial(action, side))
 
     def send_x(c):
-        return block_copy(mine, slot_x, c, at(reach_x), 0)
+        return block_copy(mine, 2, c, at(2), 0)
 
     def send_y(c):
         return block_copy(mine, slot_y, c, at(reach_y), 1)
@@ -160,14 +160,14 @@
     def send_on(c):
         return block_copy(2, slot_pass, c, sibling, 2)
 
-    def relays(c):
-        return (block_copy(carry, 2, c, at(-2), 3), block_copy(carry, 3, c, at(-1), 4))
+    def relay(c):
+        return block_copy(2, 3, c, at(1), 3)
 
     def edge_on(side):
         return edge_pass(side, 2, slot_pass, sibling, SENDS)
 
-    def edge_relays(side):
-        return (edge_pass(side, carry, 2, at(-2), SENDS + 1), edge_pass(side, carry, 3, at(-1), SENDS + 2))
+    def edge_relay(side):
+        return edge_pass(side, 2, 3, at(1), SENDS + 1)
 
     def arrived(slot, c):
         block_copy(mine, slot, c, sibling, 0).wait_recv()
@@ -176,7 +176,7 @@
         each_side(lambda side: edge_pass(side, mine, slot, sibling, 0).wait_recv())
 
     each_side(lambda side: edge_copy(side, mine, 0).start())
-    each_side(lambda side: edge_copy(side, slot_x, reach_x).start())
+    each_side(lambda side: edge_copy(side, 2, 2).start())
     pl.when(jnp.logical_not(is_d))(lambda: each_side(lambda side: edge_copy(side, slot_y, reach_y).start()))
     for c in range(CHUNKS):
         send_x(c).start()
@@ -307,25 +307,11 @@
             edge_arrived(2)
             each_side(lambda side: edge_on(side).start())
 
-            @pl.when(is_d)
-            def _():
-                edge_arrived(carry)
-
-                def hand_on(side):
-                    for copy in edge_relays(side):
-                        copy.start()
-
-                each_side(hand_on)
-
+            pl.when(is_b)(lambda: each_side(lambda side: edge_relay(side).start()))
             for c in range(CHUNKS):
                 arrived(2, c)
                 send_on(c).start()
-
-                @pl.when(is_d)
-                def _(c=c):
-                    arrived(carry, c)
-                    for copy in relays(c):
-                        copy.start()
+                pl.when(is_b)(lambda c=c: relay(c).start())
 
         @pl.when(slot != 2)
         def _():
@@ -368,7 +354,7 @@
     loop(half, apply, 8)
 
     each_side(lambda side: edge_copy(side, mine, 0).wait_send())
-    each_side(lambda side: edge_copy(side, slot_x, reach_x).wait_send())
+    each_side(lambda side: edge_copy(side, 2, 2).wait_send())
     each_side(lambda side: edge_on(side).wait_send())
     for c in range(CHUNKS):
         send_x(c).wait_send()
@@ -380,16 +366,11 @@
         for c in range(CHUNKS):
             send_y(c).wait_send()
 
-    @pl.when(is_d)
+    @pl.when(is_b)
     def _():
-        def sent(side):
-            for copy in edge_relays(side):
-                copy.wait_send()
-
-        each_side(sent)
+        each_side(lambda side: edge_relay(side).wait_send())
         for c in range(CHUNKS):
-            for copy in relays(c):
-                copy.wait_send()
+            relay(c).wait_send()
 
 
 def per_device(n_band, n_slab, orbitals, occupation):
@@ -404,7 +385,7 @@
     return pl.pallas_call(
         functools.partial(kernel, n_band, n_slab),
         out_shape=pltpu.VMEM(orbitals.shape, f32),
-        in_specs=[pl.BlockSpec(memory_space=pl.ANY), pl.BlockSpec(memory_space=pltpu.VMEM)],
+        in_specs=[pl.BlockSpec(memory_space=pl.ANY)] * 2,
         out_specs=pl.BlockSpec(memory_space=pltpu.VMEM),
         scratch_shapes=[
             pltpu.VMEM((SENDS, orbs, 2, planes, cells // 2), bf16),
@@ -417,10 +398,11 @@
             pltpu.VMEM((tiles, planes, LANES), f32),
             pltpu.VMEM((2 * LANES, 6 * LANES), bf16),
             pltpu.VMEM((3, orbs, tiles, planes, LANES), f32),
-            pltpu.SemaphoreType.DMA((2,)),
+            pltpu.VMEM(occ.shape, bf16),
+            pltpu.SemaphoreType.DMA((3,)),
             pltpu.SemaphoreType.DMA((SENDS, CHUNKS)),
             pltpu.SemaphoreType.DMA((SENDS, CHUNKS)),
-            pltpu.SemaphoreType.DMA((SENDS + 3, 2)),
+            pltpu.SemaphoreType.DMA((SENDS + 2, 2)),
             pltpu.SemaphoreType.DMA((SENDS, 2)),
         ],
         compiler_params=pltpu.CompilerParams(collective_id=0, has_side_effects=True),

time: 23.2 us -> 21.6 us (0.931)
  Pallas kernels: 22.2 us -> 20.6 us
    pallas_call x1, Pallas kernels: 22.2 us -> 20.6 us  [per_device(): pl.pallas_call(functools.partial(kernel, n_band, n_slab), out_shape=pltpu...]
where the time goes in v4:
time: 21.6 us; the launch traced here: 21.4 us
  Pallas kernels  20.6 us (95%)
  local copies, waits for them, and re-layouts  0.8 us (4%)
    pallas_call x1, Pallas kernels, per_device(): pl.pallas_call(functools.partial(kernel, n_band, n_slab), out_shape=pltpu...  20.6 us
    unnamed x1, local copies, waits for them, and re-layouts  0.8 us

profile of v4, /device:TPU:0, one launch (start us, length us, event | category | flops | bytes accessed | tf_op | source)
XLA Modules:
  0.0 21.4 jit_solution(8865052846924544017)
XLA Ops:
  0.0 20.6 %exchange.1 = f32[2,16,4096]{2,1,0:T(8,128)S(1)} custom-call(bf16[2,16,4096]{2,1,0:T(8,128)(2,1)} %orb_ref.1, bf16[1,2]{1,0:T(2,128)(2,1)} %bitcast.1), custom_call_target="tpu_custom_call" | custom-call | tf_op jit(solution)/shard_map/exchange/pallas_call | solution.py:385
  20.7 0.8 %copy.4 = f32[2,16,4096]{2,1,0:T(8,128)} copy(f32[2,16,4096]{2,1,0:T(8,128)S(1)} %exchange.1) | data formatting | bytes 1048576

commit v5 on v4

--- a/solution.py
+++ b/solution.py
@@ -35,8 +35,8 @@
 outer = (coeff_zero - coeff_two) / scale
 
 
-def loop(count, body, unroll=1):
-    lax.fori_loop(0, count, lambda i, c: (body(i), c)[1], 0, unroll=unroll)
+def loop(count, body, unroll=1, start=0):
+    lax.fori_loop(start, start + count, lambda i, c: (body(i), c)[1], 0, unroll=unroll)
 
 
 def lane_tile(t):
@@ -210,36 +210,43 @@
     def seam(value, keep_low):
         return jnp.where(low if keep_low else jnp.logical_not(low), pltpu.roll(value, NZ, 1), 0.0)
 
-    def widen(slot, dst):
-        matrix = moves[...]
+    per = half // CHUNKS
+
+    def widen(slot, dst, c):
+        pairs = range(c * per, (c + 1) * per)
+        rows = [jnp.concatenate([slots[slot, o, part, :, k * LANES:(k + 1) * LANES] for part in range(2)], axis=1)
+                for o in range(orbs) for k in pairs]
+        rows += [halos[slot, side, g] for side in range(2) for g in range(c * per // GROUP, (c + 1) * per // GROUP)]
+        moved = jnp.dot(jnp.concatenate(rows, axis=0), moves[...], preferred_element_type=jnp.float32)
+        r = 0
         for o in range(orbs):
-            stacked = jnp.concatenate(
-                [jnp.concatenate([slots[slot, o, part, :, k * LANES:(k + 1) * LANES]
-                                  for part in range(2)], axis=1) for k in range(half)], axis=0)
-            moved = jnp.dot(stacked, matrix, preferred_element_type=jnp.float32)
-            for k in range(half):
+            for k in pairs:
                 for n in range(6):
-                    dst[o, n // 2, 2 * k + n % 2 + PAD, TOP:TOP + planes] = moved[
-                        k * planes:(k + 1) * planes, n * LANES:(n + 1) * LANES]
-        for side in range(2):
-            stacked = jnp.concatenate([halos[slot, side, g] for g in range(groups)], axis=0)
-            moved = jnp.dot(stacked, matrix[:, :4 * LANES], preferred_element_type=jnp.float32)
-            to = TOP - WIDTH if side == 0 else TOP + planes
-            for k in range(half):
+                    dst[o, n // 2, 2 * k + n % 2 + PAD, TOP:TOP + planes] = moved[r:r + planes, n * LANES:(n + 1) * LANES]
+                r += planes
+        for to in (TOP - WIDTH, TOP + planes):
+            for k in pairs:
                 for o in range(orbs):
-                    r = (k * orbs + o) * WIDTH
                     for n in range(4):
                         dst[o, n // 2, 2 * k + n % 2 + PAD, to:to + WIDTH] = moved[r:r + WIDTH, n * LANES:(n + 1) * LANES]
+                    r += WIDTH
+
+    def pad_end(dst):
+        for o in range(orbs):
+            for which in range(2):
+                for n in range(PAD):
+                    dst[o, which, tiles + PAD + n] = seam(dst[o, which, PAD + n], True)
+
+    def pad_start(dst):
         for o in range(orbs):
             for which in range(2):
                 for n in range(PAD):
                     dst[o, which, n] = seam(dst[o, which, tiles + n], False)
-                    dst[o, which, tiles + PAD + n] = seam(dst[o, which, PAD + n], True)
 
     start = TOP - WIDTH
     ext = wide.shape[2]
 
-    def gather(slot, src, fresh):
+    def gather(slot, src, fresh, first, count):
         if fresh:
             rows = edges[0, groups]
         else:
@@ -263,7 +270,7 @@
                     term = w[o] * src[o, which, at_t + dy, TOP:TOP + planes]
                     value = term if value is None else value + term
                 gram[n, at_t] = value
-        loop(tiles, body, 2)
+        loop(count, body, 2 if count % 2 == 0 else 1, first)
 
     def finish(t, i):
         at_t = t + PAD
@@ -295,63 +302,105 @@
         rest[1, i, t] = back
         rest[2, i, t] = mid * flat(4)
 
-    edge_arrived(mine)
-    widen(mine, own)
-    gather(mine, own, True)
-
-    def step(n):
-        slot = jnp.where(n == 0, by_kind(3, 1, 2, 1), jnp.where(n == 1, by_kind(2, 2, 1, 2), by_kind(1, 3, 3, 3)))
+    def whole(slot, dst, fresh):
+        for c in range(CHUNKS):
+            widen(slot, dst, c)
+        pad_start(dst)
+        pad_end(dst)
+        gather(slot, dst, fresh, 0, tiles)
+
+    def edges_in(slot):
+        edge_arrived(slot)
 
         @pl.when(slot == 2)
         def _():
-            edge_arrived(2)
             each_side(lambda side: edge_on(side).start())
-
             pl.when(is_b)(lambda: each_side(lambda side: edge_relay(side).start()))
-            for c in range(CHUNKS):
-                arrived(2, c)
-                send_on(c).start()
-                pl.when(is_b)(lambda c=c: relay(c).start())
-
-        @pl.when(slot != 2)
+
+    def chunk_in(slot, c):
+        arrived(slot, c)
+
+        @pl.when(slot == 2)
         def _():
-            edge_arrived(slot)
-            for c in range(CHUNKS):
-                arrived(slot, c)
-
-        widen(slot, vis)
-        gather(slot, vis, False)
-
-    loop(STEPS, step)
-
-    for n, (which, dy) in enumerate(FLAT):
-        if dy > 0:
-            for p in range(dy):
-                gram[n, PAD - 1 - p] = seam(gram[n, PAD + tiles - 1 - p], False)
-        if dy < 0:
-            gram[n, PAD + tiles] = seam(gram[n, PAD], True)
-    for n, (which, dx, dy) in enumerate(WIDE):
-        if dy > 0:
-            wide[n, PAD - 1] = seam(wide[n, PAD + tiles - 1], False)
-        if dy < 0:
-            wide[n, PAD + tiles] = seam(wide[n, PAD], True)
-
-    def products(t):
-        for i in range(orbs):
-            finish(t, i)
-
-    loop(tiles, products)
+            send_on(c).start()
+            pl.when(is_b)(lambda: relay(c).start())
+
+    edge_arrived(mine)
+    whole(mine, own, True)
 
     def total(t, i):
         return rest[0, i, t] + pltpu.roll(rest[1, i, t], 1, 1) + pltpu.roll(rest[2, i, t], 2, 1)
 
-    def apply(k):
+    def pair_of(n):
+        return lax.rem(n + PAD + half, half)
+
+    def turn(n):
+        k = pair_of(n)
         for i in range(orbs):
-            a, b = shuffle(total(2 * k, i), total(2 * k + 1, i))
+            for h in range(2):
+                rest[0, i, 2 * k + h] = total(2 * k + h, i)
+
+    def store(n):
+        k = pair_of(n)
+        for i in range(orbs):
+            a, b = shuffle(rest[0, i, 2 * k], rest[0, i, 2 * k + 1])
             out_ref[i, :, lane_tile(k)] = a
             out_ref[i, :, lane_tile(k + half)] = b
 
-    loop(half, apply, 8)
+    def apply(n):
+        store(n - 2)
+        turn(n - 1)
+        k = pair_of(n)
+        for h in range(2):
+            for i in range(orbs):
+                finish(2 * k + h, i)
+
+    order = (by_kind(3, 1, 2, 1), by_kind(2, 2, 1, 2), by_kind(1, 3, 3, 3))
+
+    def visit(n, c):
+        slot = order[n]
+        dst = vis.at[n % 2]
+        if c == 0:
+            edges_in(slot)
+        chunk_in(slot, c)
+        widen(slot, dst, c)
+        if c == 0:
+            pad_end(dst)
+        first = 2 * per * c - PAD if c else 1
+        final = c == CHUNKS - 1
+        gather(slot, dst, False, first, (tiles if final else 2 * per * (c + 1) - PAD) - first)
+        if final:
+            pad_start(dst)
+            gather(slot, dst, False, 0, 1)
+
+    applied = 0
+    for c in range(CHUNKS):
+        visit(0, c)
+    visit(1, 0)
+    for c in range(CHUNKS):
+        final = c == CHUNKS - 1
+        if not final:
+            visit(1, c + 1)
+        visit(2, c)
+        if final:
+            for n, (which, dy) in enumerate(FLAT):
+                if dy > 0:
+                    for p in range(dy):
+                        gram[n, PAD - 1 - p] = seam(gram[n, PAD + tiles - 1 - p], False)
+                if dy < 0:
+                    gram[n, PAD + tiles] = seam(gram[n, PAD], True)
+            for n, (which, dx, dy) in enumerate(WIDE):
+                if dy > 0:
+                    wide[n, PAD - 1] = seam(wide[n, PAD + tiles - 1], False)
+                if dy < 0:
+                    wide[n, PAD + tiles] = seam(wide[n, PAD], True)
+        done = half if final else max((2 * per * (c + 1) - PAD - 1) // 2 - PAD, 0)
+        if done > applied:
+            loop(done - applied, apply, 1, applied)
+        applied = done
+    store(half - 2)
+    turn(half - 1)
+    store(half - 1)
 
     each_side(lambda side: edge_copy(side, mine, 0).wait_send())
     each_side(lambda side: edge_copy(side, 2, 2).wait_send())
@@ -377,11 +426,11 @@
     orbs, planes, cells = orbitals.shape
     tiles = cells // LANES
     ext = -(-(planes + 2 * WIDTH) // 8) * 8
-    tall = planes + 2 * TOP
+    tall = planes + 2 * TOP + 8
     occ = occupation.reshape(1, orbs)
     f32, bf16 = jnp.float32, jnp.bfloat16
     rows, groups = GROUP * orbs * WIDTH, tiles // (2 * GROUP)
-    padded = tiles + 2 * PAD
+    padded = tiles + 2 * PAD + 1
     return pl.pallas_call(
         functools.partial(kernel, n_band, n_slab),
         out_shape=pltpu.VMEM(orbitals.shape, f32),
@@ -392,7 +441,7 @@
             pltpu.VMEM((2, groups + 1, rows, 2 * LANES), bf16),
             pltpu.VMEM((SENDS, 2, groups + 1, rows, 2 * LANES), bf16),
             pltpu.VMEM((orbs, 3, padded, tall, LANES), f32),
-            pltpu.VMEM((orbs, 3, padded, tall, LANES), f32),
+            pltpu.VMEM((2, orbs, 3, padded, tall, LANES), f32),
             pltpu.VMEM((len(FLAT), padded, planes, LANES), f32),
             pltpu.VMEM((len(WIDE), padded, ext, LANES), f32),
             pltpu.VMEM((tiles, planes, LANES), f32),

time: 21.6 us -> 20.2 us (0.935)
  Pallas kernels: 20.6 us -> 19.3 us
    pallas_call x1, Pallas kernels: 20.6 us -> 19.3 us  [per_device(): pl.pallas_call(functools.partial(kernel, n_band, n_slab), out_shape=pltpu...]
where the time goes in v5:
time: 20.2 us; the launch traced here: 20.1 us
  Pallas kernels  19.3 us (96%)
  local copies, waits for them, and re-layouts  0.8 us (4%)
    pallas_call x1, Pallas kernels, per_device(): pl.pallas_call(functools.partial(kernel, n_band, n_slab), out_shape=pltpu...  19.3 us
    unnamed x1, local copies, waits for them, and re-layouts  0.8 us

profile of v5, /device:TPU:0, one launch (start us, length us, event | category | flops | bytes accessed | tf_op | source)
XLA Modules:
  0.0 20.1 jit_solution(17198382730288066792)
XLA Ops:
  0.0 19.3 %exchange.1 = f32[2,16,4096]{2,1,0:T(8,128)S(1)} custom-call(bf16[2,16,4096]{2,1,0:T(8,128)(2,1)} %orb_ref.1, bf16[1,2]{1,0:T(2,128)(2,1)} %bitcast.1), custom_call_target="tpu_custom_call" | custom-call | tf_op jit(solution)/shard_map/exchange/pallas_call | solution.py:434
  19.3 0.8 %copy.4 = f32[2,16,4096]{2,1,0:T(8,128)} copy(f32[2,16,4096]{2,1,0:T(8,128)S(1)} %exchange.1) | data formatting | bytes 1048576

commit v6 on v5

--- a/solution.py
+++ b/solution.py
@@ -14,7 +14,8 @@
 WIDTH = 2
 PAD = 2
 GROUP = 4
-CHUNKS = 4
+CUTS = (0, 4, 8, 12, 16)
+CHUNKS = len(CUTS) - 1
 SENDS = STEPS + 1
 TOP = 8
 FLAT = ((0, 0), (0, 1), (0, 2), (1, 0), (2, 0), (1, 1), (1, -1))
@@ -44,13 +45,13 @@
 
 
 def kernel(n_band, n_slab, orb_ref, occ_ref, out_ref, slots, edges, halos, own, vis, gram, wide, centre,
-           moves, rest, occ, load_sem, send_sem, recv_sem, edge_send, edge_recv):
+           moves, rest, occ, factors, load_sem, send_sem, recv_sem, edge_send, edge_recv):
     orbs, planes, cells = orb_ref.shape
     tiles = cells // LANES
     half = tiles // 2
     groups = half // GROUP
     mine = 0
-    chunk = half * LANES // CHUNKS
+    bounds = [half * n // CUTS[-1] for n in CUTS]
     band, slab = lax.axis_index("band"), lax.axis_index("slab")
     kind = lax.rem(band, 4)
     is_b, is_d = kind == 1, kind == 3
@@ -102,6 +103,57 @@
 
     for load in loads:
         load.wait()
+    pl.semaphore_wait(barrier, by_kind(2, 4, 2, 2) + sides * by_kind(3, 3, 3, 2))
+
+    def edge_copy(side, slot, by):
+        return pltpu.make_async_remote_copy(
+            src_ref=edges.at[side], dst_ref=halos.at[slot, 1 - side],
+            send_sem=edge_send.at[slot, side], recv_sem=edge_recv.at[slot, 1 - side],
+            device_id=at(by, step_of[side]), device_id_type=MESH)
+
+    def edge_pass(side, src, slot, device, sem):
+        return pltpu.make_async_remote_copy(
+            src_ref=halos.at[src, side], dst_ref=halos.at[slot, side],
+            send_sem=edge_send.at[sem, side], recv_sem=edge_recv.at[slot, side],
+            device_id=device, device_id_type=MESH)
+
+    def piece(ref, slot, c):
+        return ref.at[slot, :, :, :, bounds[c] * LANES:bounds[c + 1] * LANES]
+
+    def block_copy(src, slot, c, device, sem):
+        return pltpu.make_async_remote_copy(
+            src_ref=piece(slots, src, c), dst_ref=piece(slots, slot, c), send_sem=send_sem.at[sem, c],
+            recv_sem=recv_sem.at[slot, c], device_id=device, device_id_type=MESH)
+
+    def each_side(action):
+        for side in range(2):
+            pl.when(has[side])(functools.partial(action, side))
+
+    def send_x(c):
+        return block_copy(mine, 2, c, at(2), 0)
+
+    def send_y(c):
+        return block_copy(mine, slot_y, c, at(reach_y), 1)
+
+    def send_on(c):
+        return block_copy(2, slot_pass, c, sibling, 2)
+
+    def relay(c):
+        return block_copy(2, 3, c, at(1), 3)
+
+    def edge_on(side):
+        return edge_pass(side, 2, slot_pass, sibling, SENDS)
+
+    def edge_relay(side):
+        return edge_pass(side, 2, 3, at(1), SENDS + 1)
+
+    def arrived(slot, c):
+        block_copy(mine, slot, c, sibling, 0).wait_recv()
+
+    def edge_arrived(slot):
+        each_side(lambda side: edge_pass(side, mine, slot, sibling, 0).wait_recv())
+
+    send_x(0).start()
     for side in range(2):
         rows = [jnp.broadcast_to(occ[:, o:o + 1].astype(jnp.float32), (1, 2 * LANES)) for o in range(orbs)]
         rows.append(jnp.zeros((edges.shape[2] - orbs, 2 * LANES), jnp.float32))
@@ -125,61 +177,12 @@
         def _(side=side):
             halos[:, side] = jnp.zeros(halos.shape[:1] + halos.shape[2:], jnp.bfloat16)
 
-    pl.semaphore_wait(barrier, by_kind(2, 4, 2, 2) + sides * by_kind(3, 3, 3, 2))
-
-    def edge_copy(side, slot, by):
-        return pltpu.make_async_remote_copy(
-            src_ref=edges.at[side], dst_ref=halos.at[slot, 1 - side],
-            send_sem=edge_send.at[slot, side], recv_sem=edge_recv.at[slot, 1 - side],
-            device_id=at(by, step_of[side]), device_id_type=MESH)
-
-    def edge_pass(side, src, slot, device, sem):
-        return pltpu.make_async_remote_copy(
-            src_ref=halos.at[src, side], dst_ref=halos.at[slot, side],
-            send_sem=edge_send.at[sem, side], recv_sem=edge_recv.at[slot, side],
-            device_id=device, device_id_type=MESH)
-
-    def piece(ref, slot, c):
-        return ref.at[slot, :, :, :, c * chunk:(c + 1) * chunk]
-
-    def block_copy(src, slot, c, device, sem):
-        return pltpu.make_async_remote_copy(
-            src_ref=piece(slots, src, c), dst_ref=piece(slots, slot, c), send_sem=send_sem.at[sem, c],
-            recv_sem=recv_sem.at[slot, c], device_id=device, device_id_type=MESH)
-
-    def each_side(action):
-        for side in range(2):
-            pl.when(has[side])(functools.partial(action, side))
-
-    def send_x(c):
-        return block_copy(mine, 2, c, at(2), 0)
-
-    def send_y(c):
-        return block_copy(mine, slot_y, c, at(reach_y), 1)
-
-    def send_on(c):
-        return block_copy(2, slot_pass, c, sibling, 2)
-
-    def relay(c):
-        return block_copy(2, 3, c, at(1), 3)
-
-    def edge_on(side):
-        return edge_pass(side, 2, slot_pass, sibling, SENDS)
-
-    def edge_relay(side):
-        return edge_pass(side, 2, 3, at(1), SENDS + 1)
-
-    def arrived(slot, c):
-        block_copy(mine, slot, c, sibling, 0).wait_recv()
-
-    def edge_arrived(slot):
-        each_side(lambda side: edge_pass(side, mine, slot, sibling, 0).wait_recv())
-
     each_side(lambda side: edge_copy(side, mine, 0).start())
     each_side(lambda side: edge_copy(side, 2, 2).start())
     pl.when(jnp.logical_not(is_d))(lambda: each_side(lambda side: edge_copy(side, slot_y, reach_y).start()))
     for c in range(CHUNKS):
-        send_x(c).start()
+        if c > 0:
+            send_x(c).start()
         pl.when(jnp.logical_not(is_d))(lambda c=c: send_y(c).start())
 
     def prepare(t):
@@ -210,13 +213,12 @@
     def seam(value, keep_low):
         return jnp.where(low if keep_low else jnp.logical_not(low), pltpu.roll(value, NZ, 1), 0.0)
 
-    per = half // CHUNKS
-
     def widen(slot, dst, c):
-        pairs = range(c * per, (c + 1) * per)
+        pairs = range(bounds[c], bounds[c + 1])
+        near = range(bounds[c] // GROUP, -(-bounds[c + 1] // GROUP))
         rows = [jnp.concatenate([slots[slot, o, part, :, k * LANES:(k + 1) * LANES] for part in range(2)], axis=1)
                 for o in range(orbs) for k in pairs]
-        rows += [halos[slot, side, g] for side in range(2) for g in range(c * per // GROUP, (c + 1) * per // GROUP)]
+        rows += [halos[slot, side, g] for side in range(2) for g in near]
         moved = jnp.dot(jnp.concatenate(rows, axis=0), moves[...], preferred_element_type=jnp.float32)
         r = 0
         for o in range(orbs):
@@ -225,9 +227,9 @@
                     dst[o, n // 2, 2 * k + n % 2 + PAD, TOP:TOP + planes] = moved[r:r + planes, n * LANES:(n + 1) * LANES]
                 r += planes
         for to in (TOP - WIDTH, TOP + planes):
-            for k in pairs:
+            for k in range(near[0] * GROUP, (near[-1] + 1) * GROUP):
                 for o in range(orbs):
-                    for n in range(4):
+                    for n in range(4 if k in pairs else 0):
                         dst[o, n // 2, 2 * k + n % 2 + PAD, to:to + WIDTH] = moved[r:r + WIDTH, n * LANES:(n + 1) * LANES]
                     r += WIDTH
 
@@ -246,13 +248,17 @@
     start = TOP - WIDTH
     ext = wide.shape[2]
 
-    def gather(slot, src, fresh, first, count):
+    def weigh(slot, fresh):
         if fresh:
             rows = edges[0, groups]
         else:
             rows = jnp.where(has[0], halos[slot, 0, groups].astype(jnp.float32), halos[slot, 1, groups].astype(jnp.float32))
         rows = -scale * rows[:orbs, :LANES].astype(jnp.float32)
-        weights = [jnp.broadcast_to(rows[o:o + 1], (ext, LANES)) for o in range(orbs)]
+        for o in range(orbs):
+            factors[slot, o] = jnp.broadcast_to(rows[o:o + 1], (8, LANES))
+
+    def gather(slot, src, fresh, first, count):
+        weights = [jnp.concatenate([factors[slot, o]] * (ext // 8), axis=0) for o in range(orbs)]
 
         def body(t):
             at_t = t + PAD
@@ -270,7 +276,7 @@
                     term = w[o] * src[o, which, at_t + dy, TOP:TOP + planes]
                     value = term if value is None else value + term
                 gram[n, at_t] = value
-        loop(count, body, 2 if count % 2 == 0 else 1, first)
+        loop(count, body, count if count < tiles else 4, first)
 
     def finish(t, i):
         at_t = t + PAD
@@ -326,6 +332,7 @@
             pl.when(is_b)(lambda: relay(c).start())
 
     edge_arrived(mine)
+    weigh(mine, True)
     whole(mine, own, True)
 
     def total(t, i):
@@ -362,16 +369,31 @@
         dst = vis.at[n % 2]
         if c == 0:
             edges_in(slot)
+            weigh(slot, False)
         chunk_in(slot, c)
         widen(slot, dst, c)
         if c == 0:
             pad_end(dst)
-        first = 2 * per * c - PAD if c else 1
+        first = 2 * bounds[c] - PAD if c else 1
         final = c == CHUNKS - 1
-        gather(slot, dst, False, first, (tiles if final else 2 * per * (c + 1) - PAD) - first)
+        gather(slot, dst, False, first, (tiles if final else 2 * bounds[c + 1] - PAD) - first)
         if final:
             pad_start(dst)
             gather(slot, dst, False, 0, 1)
+
+    def direct_sent():
+        each_side(lambda side: edge_copy(side, mine, 0).wait_send())
+        each_side(lambda side: edge_copy(side, 2, 2).wait_send())
+        each_side(lambda side: edge_on(side).wait_send())
+        pl.when(is_b)(lambda: each_side(lambda side: edge_relay(side).wait_send()))
+        for c in range(CHUNKS):
+            send_x(c).wait_send()
+
+        @pl.when(jnp.logical_not(is_d))
+        def _():
+            each_side(lambda side: edge_copy(side, slot_y, reach_y).wait_send())
+            for c in range(CHUNKS):
+                send_y(c).wait_send()
 
     applied = 0
     for c in range(CHUNKS):
@@ -381,6 +403,8 @@
         final = c == CHUNKS - 1
         if not final:
             visit(1, c + 1)
+        else:
+            direct_sent()
         visit(2, c)
         if final:
             for n, (which, dy) in enumerate(FLAT):
@@ -394,7 +418,7 @@
                     wide[n, PAD - 1] = seam(wide[n, PAD + tiles - 1], False)
                 if dy < 0:
                     wide[n, PAD + tiles] = seam(wide[n, PAD], True)
-        done = half if final else max((2 * per * (c + 1) - PAD - 1) // 2 - PAD, 0)
+        done = half if final else max((2 * bounds[c + 1] - PAD - 1) // 2 - PAD, 0)
         if done > applied:
             loop(done - applied, apply, 1, applied)
         applied = done
@@ -402,24 +426,10 @@
     turn(half - 1)
     store(half - 1)
 
-    each_side(lambda side: edge_copy(side, mine, 0).wait_send())
-    each_side(lambda side: edge_copy(side, 2, 2).wait_send())
-    each_side(lambda side: edge_on(side).wait_send())
     for c in range(CHUNKS):
-        send_x(c).wait_send()
         send_on(c).wait_send()
 
-    @pl.when(jnp.logical_not(is_d))
-    def _():
-        each_side(lambda side: edge_copy(side, slot_y, reach_y).wait_send())
-        for c in range(CHUNKS):
-            send_y(c).wait_send()
-
-    @pl.when(is_b)
-    def _():
-        each_side(lambda side: edge_relay(side).wait_send())
-        for c in range(CHUNKS):
-            relay(c).wait_send()
+        pl.when(is_b)(lambda c=c: relay(c).wait_send())
 
 
 def per_device(n_band, n_slab, orbitals, occupation):
@@ -430,7 +440,7 @@
     occ = occupation.reshape(1, orbs)
     f32, bf16 = jnp.float32, jnp.bfloat16
     rows, groups = GROUP * orbs * WIDTH, tiles // (2 * GROUP)
-    padded = tiles + 2 * PAD + 1
+    padded = tiles + 2 * PAD
     return pl.pallas_call(
         functools.partial(kernel, n_band, n_slab),
         out_shape=pltpu.VMEM(orbitals.shape, f32),
@@ -448,6 +458,7 @@
             pltpu.VMEM((2 * LANES, 6 * LANES), bf16),
             pltpu.VMEM((3, orbs, tiles, planes, LANES), f32),
             pltpu.VMEM(occ.shape, bf16),
+            pltpu.VMEM((SENDS, orbs, 8, LANES), f32),
             pltpu.SemaphoreType.DMA((3,)),
             pltpu.SemaphoreType.DMA((SENDS, CHUNKS)),
             pltpu.SemaphoreType.DMA((SENDS, CHUNKS)),

time: 20.2 us -> 19.4 us (0.960)
  Pallas kernels: 19.3 us -> 18.5 us
    pallas_call x1, Pallas kernels: 19.3 us -> 18.5 us  [per_device(): pl.pallas_call(functools.partial(kernel, n_band, n_slab), out_shape=pltpu...]
where the time goes in v6:
time: 19.4 us; the launch traced here: 19.3 us
  Pallas kernels  18.5 us (95%)
  local copies, waits for them, and re-layouts  0.8 us (4%)
    pallas_call x1, Pallas kernels, per_device(): pl.pallas_call(functools.partial(kernel, n_band, n_slab), out_shape=pltpu...  18.5 us
    unnamed x1, local copies, waits for them, and re-layouts  0.8 us

profile of v6, /device:TPU:0, one launch (start us, length us, event | category | flops | bytes accessed | tf_op | source)
XLA Modules:
  0.0 19.3 jit_solution(13832871869948042046)
XLA Ops:
  0.0 18.5 %exchange.1 = f32[2,16,4096]{2,1,0:T(8,128)S(1)} custom-call(bf16[2,16,4096]{2,1,0:T(8,128)(2,1)} %orb_ref.1, bf16[1,2]{1,0:T(2,128)(2,1)} %bitcast.1), custom_call_target="tpu_custom_call" | custom-call | tf_op jit(solution)/shard_map/exchange/pallas_call | solution.py:444
  18.5 0.8 %copy.4 = f32[2,16,4096]{2,1,0:T(8,128)} copy(f32[2,16,4096]{2,1,0:T(8,128)S(1)} %exchange.1) | data formatting | bytes 1048576

commit v7 on v6

--- a/solution.py
+++ b/solution.py
@@ -420,7 +420,7 @@
                     wide[n, PAD + tiles] = seam(wide[n, PAD], True)
         done = half if final else max((2 * bounds[c + 1] - PAD - 1) // 2 - PAD, 0)
         if done > applied:
-            loop(done - applied, apply, 1, applied)
+            loop(done - applied, apply, done - applied, applied)
         applied = done
     store(half - 2)
     turn(half - 1)

time: 19.4 us -> 18.7 us (0.964)
  Pallas kernels: 18.5 us -> 17.7 us
    pallas_call x1, Pallas kernels: 18.5 us -> 17.7 us  [per_device(): pl.pallas_call(functools.partial(kernel, n_band, n_slab), out_shape=pltpu...]
where the time goes in v7:
time: 18.7 us; the launch traced here: 18.6 us
  Pallas kernels  17.7 us (95%)
  local copies, waits for them, and re-layouts  0.8 us (4%)
    pallas_call x1, Pallas kernels, per_device(): pl.pallas_call(functools.partial(kernel, n_band, n_slab), out_shape=pltpu...  17.7 us
    unnamed x1, local copies, waits for them, and re-layouts  0.8 us

profile of v7, /device:TPU:0, one launch (start us, length us, event | category | flops | bytes accessed | tf_op | source)
XLA Modules:
  0.0 18.6 jit_solution(3342514783273664686)
XLA Ops:
  0.0 17.7 %exchange.1 = f32[2,16,4096]{2,1,0:T(8,128)S(1)} custom-call(bf16[2,16,4096]{2,1,0:T(8,128)(2,1)} %orb_ref.1, bf16[1,2]{1,0:T(2,128)(2,1)} %bitcast.1), custom_call_target="tpu_custom_call" | custom-call | tf_op jit(solution)/shard_map/exchange/pallas_call | solution.py:444
  17.8 0.8 %copy.4 = f32[2,16,4096]{2,1,0:T(8,128)} copy(f32[2,16,4096]{2,1,0:T(8,128)S(1)} %exchange.1) | data formatting | bytes 1048576
